TPU v7x, 512 devices: a whole 4x4x16 slice. The times are simulated.
512 devices in a mesh: dp: 32 (over z, core), vocab: 16 (over y, x).
Axes of the slice: x: 4, y: 4, z: 16, core: 2. Of those that a mesh axis runs over, the one named last changes fastest.
Arguments:
- hidden: float32 [64, 2, 32, 4096], P('dp', None, None, 'vocab'), may hold values from -64 to 64, as said below
- head_weight: float32 [4096, 4096], P(None, 'vocab'), may hold values from -1 to 1, as said below
- targets: int32 [64, 2, 32], P('dp'), may hold values from 0 to 4095
- lengths: int32 [64, 2], P('dp'), may hold values from 8 to 32
- rest_lse: float32 [64, 2, 32], P('dp'), may hold values from 6 to 10
- ref_logp: float32 [64, 2], P('dp'), may hold values from -120 to 120
- group_map: int32 [64], P('dp'), may hold values from 0 to 31, as said below
- group_weight: float32 [32], replicated, may hold values from 0.25 to 4
Outputs:
- hidden_grad: float32 [64, 2, 32, 4096], P('dp', None, None, 'vocab')
- dpo_loss: float32 [], replicated
Inputs may be any that keep to these rules, and one draw needn't show every extreme that they name: `hidden`: standard normal states; in some draws a few tokens lie near large multiples of two head columns. `head_weight`: entries of order one over the square root of 4096. `group_map`: each pair names its own group or one of the two next to it (indices modulo 32); every group is named by exactly 2 pairs, and at most one pair of a group names each neighbour.
All inputs are finite; a program needn't handle non-finite values.
Results may differ from a plain program's by a relative error of at most 0.0003.
Values sent between devices are 32-bit elements; how exact they have to be, the bound alone decides.
No kernel may reach another device: no remote copies, remote signals or barrier semaphores. Data moves between devices by JAX's collectives and lax.ppermute only.
A program may use at most 64 MiB of HBM per device.

v0:
```python
import jax
import jax.numpy as jnp
from jax import lax
from jax.experimental import pallas as pl
from jax.experimental.pallas import tpu as pltpu
from jax.sharding import PartitionSpec as P

beta_scale = 0.05
both_axes = ("dp", "vocab")
near_members = 8
stat_rows = 8
vmem_grant = 24 * 1024 * 1024


def near_groups(pairs, holders):
    return [
        [(block + k) * holders + place for k in range(near_members)]
        for block in range(0, pairs, near_members)
        for place in range(holders)
    ]


def far_groups(pairs, holders):
    return [
        [(block + k) * holders + place for block in range(0, pairs, near_members)]
        for k in range(near_members)
        for place in range(holders)
    ]


def split_parts(values):
    high = values.astype(jnp.bfloat16)
    low = (values - high.astype(jnp.float32)).astype(jnp.bfloat16)
    return high, low


def stacked_parts(values):
    return jnp.concatenate(split_parts(values), axis=0)


def product(both, weight, weight_dim):
    rows = both.shape[0] // 2
    high, low = split_parts(weight)
    dims = (((1,), (weight_dim,)), ((), ()))
    wide = lax.dot_general(both, high, dims, preferred_element_type=jnp.float32)
    narrow = lax.dot_general(both[:rows], low, dims, preferred_element_type=jnp.float32)
    return wide[:rows] + (wide[rows:] + narrow)


def column_matches(target_row, base, columns):
    ids = base + lax.broadcasted_iota(jnp.int32, (columns, target_row.shape[1]), 0)
    return ids == target_row


def copies_kernel(shard_ref, base_ref, target_ref, outside_ref, out_ref):
    shard = shard_ref[...]
    for k in range(out_ref.shape[0]):
        out_ref[k] = shard


def copies_for_all(shard, holders, base, target_row, outside_row):
    return pl.pallas_call(
        copies_kernel,
        out_shape=jax.ShapeDtypeStruct((holders, *shard.shape), shard.dtype),
        in_specs=[pl.BlockSpec(memory_space=pltpu.VMEM), pl.BlockSpec(memory_space=pltpu.SMEM)]
        + [pl.BlockSpec(memory_space=pltpu.VMEM)] * 2,
        out_specs=pl.BlockSpec(memory_space=pltpu.VMEM),
        compiler_params=pltpu.CompilerParams(vmem_limit_bytes=vmem_grant),
        name="state_copies",
    )(shard, base, target_row, outside_row)


def logits_kernel(base_ref, states_ref, target_ref, weight_ref, scaled_ref, own_ref, stats_ref):
    total = product(stacked_parts(states_ref[0]), weight_ref[0], 0)
    for k in range(1, states_ref.shape[0]):
        total += product(stacked_parts(states_ref[k]), weight_ref[k], 0)
    logits = total.T
    peak = jnp.max(logits, axis=0, keepdims=True)
    scaled = jnp.exp(logits - peak)
    scaled_ref[...] = scaled
    matches = column_matches(target_ref[...], base_ref[0], logits.shape[0])
    exponentials = jnp.sum(scaled, axis=0, keepdims=True)
    target = jnp.sum(jnp.where(matches, logits, 0.0), axis=0, keepdims=True)
    row = lax.broadcasted_iota(jnp.int32, own_ref.shape, 0)
    stats = jnp.where(row == 0, peak, jnp.where(row == 1, exponentials, target))
    own_ref[...] = stats
    for k in range(stats_ref.shape[0]):
        stats_ref[k] = stats


def local_logits(base, states, target_row, weight_blocks):
    holders, tokens, _ = states.shape
    columns = weight_blocks.shape[2]
    return pl.pallas_call(
        logits_kernel,
        out_shape=(
            jax.ShapeDtypeStruct((columns, tokens), jnp.float32),
            jax.ShapeDtypeStruct((stat_rows, tokens), jnp.float32),
            jax.ShapeDtypeStruct((holders, stat_rows, tokens), jnp.float32),
        ),
        in_specs=[
            pl.BlockSpec(memory_space=pltpu.SMEM),
            pl.BlockSpec(memory_space=pltpu.VMEM),
            pl.BlockSpec(memory_space=pltpu.VMEM),
            pl.BlockSpec(memory_space=pltpu.VMEM),
        ],
        out_specs=(pl.BlockSpec(memory_space=pltpu.VMEM),) * 3,
        compiler_params=pltpu.CompilerParams(vmem_limit_bytes=vmem_grant),
        cost_estimate=pl.CostEstimate(
            flops=6 * states.size * columns,
            bytes_accessed=4 * (states.size + weight_blocks.size),
            transcendentals=tokens * columns,
        ),
        name="local_logits",
    )(base, states, target_row, weight_blocks)


def softplus(values):
    small = jnp.exp(-jnp.abs(values))
    shifted = 1.0 + small
    gap = shifted - 1.0
    safe = jnp.where(gap == 0.0, 1.0, gap)
    log_shifted = jnp.where(gap == 0.0, small, jnp.log(shifted) * (small / safe))
    return jnp.maximum(values, 0.0) + log_shifted


def rows_kernel(
    base_ref,
    lengths_ref,
    ref_logp_ref,
    group_map_ref,
    weight_of_ref,
    stats_ref,
    own_ref,
    scaled_ref,
    target_ref,
    outside_ref,
    weight_ref,
    rows_ref,
    loss_ref,
    made_ref,
    sems,
):
    pair_count, seq_slots = lengths_ref.shape[0], target_ref.shape[1] // lengths_ref.size
    stats = stats_ref[...]
    peaks, totals, targets = (stats[:, k : k + 1] for k in range(3))
    row_peak = jnp.max(peaks, axis=0)
    row_total = jnp.sum(totals * jnp.exp(peaks - row_peak[None]), axis=0)
    target_logit = jnp.sum(targets, axis=0)
    window_lse = row_peak + jnp.log(row_total)
    outside = outside_ref[...]
    ceiling = jnp.maximum(window_lse, outside)
    full_lse = ceiling + jnp.log(jnp.exp(window_lse - ceiling) + jnp.exp(outside - ceiling))

    token = lax.broadcasted_iota(jnp.int32, outside.shape, 1)
    slot, sequence = token % seq_slots, token // seq_slots
    divisor = 0.0
    for k in range(weight_of_ref.shape[0]):
        divisor += weight_of_ref[k]
    divisor = pair_count * divisor
    token_grad = jnp.zeros(outside.shape, jnp.float32)
    loss = jnp.zeros((1, 1), jnp.float32)
    for pair in range(pair_count):
        scores, masks = [], []
        for one in range(2):
            live = (sequence == 2 * pair + one) & (slot < lengths_ref[pair, one])
            kept = jnp.where(live, target_logit - full_lse, 0.0)
            scores.append(jnp.sum(kept, axis=1, keepdims=True) - ref_logp_ref[pair, one])
            masks.append(live)
        margin = beta_scale * (scores[0] - scores[1])
        pair_weight = weight_of_ref[group_map_ref[pair]]
        loss += pair_weight * softplus(-margin) / divisor
        coefficient = -beta_scale * pair_weight / (1.0 + jnp.exp(margin)) / divisor
        token_grad += jnp.where(masks[0], coefficient, 0.0)
        token_grad -= jnp.where(masks[1], coefficient, 0.0)
    loss_ref[...] = jnp.broadcast_to(loss, loss_ref.shape)

    scale = jnp.exp(own_ref[0:1] - full_lse)
    matches = column_matches(target_ref[...], base_ref[0], scaled_ref.shape[0])
    grad = token_grad * (matches.astype(jnp.float32) - scale * scaled_ref[...])
    both = stacked_parts(grad.T)
    sent = []
    for k in range(made_ref.shape[0]):
        made_ref[k] = product(both, weight_ref[k], 1)
        sent.append(pltpu.make_async_copy(made_ref.at[k], rows_ref.at[k], sems.at[k]))
        sent[k].start()
    for copy in sent:
        copy.wait()


def gradient_rows(scalars, arrays, weight_blocks, tokens):
    holders, width, columns = weight_blocks.shape
    rows_shape = (holders, tokens, width)
    return pl.pallas_call(
        rows_kernel,
        out_shape=(
            pltpu.HBM(rows_shape, jnp.float32),
            jax.ShapeDtypeStruct((1, tokens), jnp.float32),
        ),
        in_specs=[pl.BlockSpec(memory_space=pltpu.SMEM)] * len(scalars)
        + [pl.BlockSpec(memory_space=pltpu.VMEM)] * (len(arrays) + 1),
        out_specs=(pl.BlockSpec(memory_space=pltpu.HBM), pl.BlockSpec(memory_space=pltpu.VMEM)),
        scratch_shapes=[pltpu.VMEM(rows_shape, jnp.float32), pltpu.SemaphoreType.DMA((holders,))],
        compiler_params=pltpu.CompilerParams(vmem_limit_bytes=vmem_grant),
        cost_estimate=pl.CostEstimate(
            flops=6 * tokens * weight_blocks.size,
            bytes_accessed=4 * (holders * tokens * width + weight_blocks.size),
            transcendentals=tokens * holders,
        ),
        name="gradient_rows",
    )(*scalars, *arrays, weight_blocks)


def shards(hidden, head_weight, targets, lengths, rest_lse, ref_logp, group_map, group_weight):
    pair_count, _, seq_slots, local_width = hidden.shape
    column_count = head_weight.shape[1]
    pairs, holders = lax.axis_size("dp"), lax.axis_size("vocab")
    tokens = pair_count * 2 * seq_slots
    weight_blocks = head_weight.reshape(holders, local_width, column_count)
    base = (lax.axis_index("vocab") * column_count).astype(jnp.int32).reshape(1)
    target_row = targets.reshape(1, tokens)
    outside_row = rest_lse.reshape(1, tokens)

    state_copies = copies_for_all(
        hidden.reshape(tokens, local_width), holders, base, target_row, outside_row
    )
    states = lax.all_to_all(state_copies, "vocab", 0, 0, tiled=True)
    scaled, own_stats, stat_copies = local_logits(base, states, target_row, weight_blocks)
    stats = lax.all_to_all(stat_copies, "vocab", 0, 0, tiled=True)
    partial_rows, loss_row = gradient_rows(
        (base, lengths, ref_logp, group_map, group_weight),
        (stats, own_stats, scaled, target_row, outside_row),
        weight_blocks,
        tokens,
    )
    summed_rows = jnp.sum(lax.all_to_all(partial_rows, "vocab", 0, 0, tiled=True), axis=0)
    loss_row = lax.psum(loss_row, both_axes, axis_index_groups=near_groups(pairs, holders))
    loss_row = lax.psum(loss_row, both_axes, axis_index_groups=far_groups(pairs, holders))
    return (summed_rows.reshape(hidden.shape), loss_row[0, 0])


def solution(mesh):
    return jax.shard_map(
        shards,
        mesh=mesh,
        in_specs=(
            P("dp", None, None, "vocab"),
            P(None, "vocab"),
            P("dp", None, None),
            P("dp", None),
            P("dp", None, None),
            P("dp", None),
            P("dp"),
            P(),
        ),
        out_specs=(P("dp", None, None, "vocab"), P()),
        check_vma=False,
    )
```

profile of v0, /device:TPU:4, one launch (start us, length us, event | category | flops | bytes accessed | tf_op | source)
XLA Modules:
  0.0 94.6 jit_solution(787230083000931812)
XLA Ops:
  0.6 0.8 reshape.24.target_ref
  1.4 0.8 reshape.25.outside_ref
  2.2 0.0 copy-start.1
  2.2 0.9 copy-done.1
  3.1 0.2 state_copies.1
  3.3 0.0 copy-start
  3.3 33.7 %all_to_all.15.states_ref = f32[16,128,256]{2,1,0:T(8,128)S(1)} all-to-all(f32[16,128,256]{2,1,0:T(8,128)S(1)} %state_copies.1), channel_id=1, replica_groups=mesh['dp'=32,'vocab'=16] {'vocab'}, dimensions={0} | all-to-all | bytes 4194304 | tf_op jit(solution)/shard_map/all_to_all | solution.py:227
  37.0 0.0 copy-done
  37.0 0.0 copy-start.2
  37.0 0.0 copy-start.3
  37.0 0.0 copy-start.4
  37.0 0.0 copy-start.5
  37.1 1.3 %local_logits.1 = (f32[256,128]{1,0:T(8,128)S(1)}, f32[8,128]{1,0:T(8,128)S(1)}, f32[16,8,128]{2,1,0:T(8,128)S(1)}) custom-call(s32[1]{0:T(128)} %bitcast.base_ref, f32[16,128,256]{2,1,0:T(8,128)S(1)} %all_to_all.15.states_ref, s32[1,128]{1,0:T(1,128)S(1)} %reshape.24.target_ref, f32[16,256,256]{2,1,0:T(8,128)S(1)} %bitcast.6), custom_call_target="tpu_custom_call" | custom-call | flops 805306368 | bytes 6291456 | tf_op jit(solution)/shard_map/local_logits/pallas_call | solution.py:94
  38.4 10.8 %all_to_all.16.stats_ref = f32[16,8,128]{2,1,0:T(8,128)S(1)} all-to-all(f32[16,8,128]{2,1,0:T(8,128)S(1)} %get-tuple-element.7), channel_id=1, replica_groups=mesh['dp'=32,'vocab'=16] {'vocab'}, dimensions={0} | all-to-all | bytes 131072 | tf_op jit(solution)/shard_map/all_to_all | solution.py:229
  49.2 0.0 copy-done.2
  49.2 0.0 copy-done.3
  49.2 0.0 copy-done.4
  49.2 0.0 copy-done.5
  49.2 3.1 %gradient_rows.1 = (f32[16,128,256]{2,1,0:T(8,128)}, f32[1,128]{1,0:T(1,128)S(1)}) custom-call(s32[1]{0:T(128)} %bitcast.base_ref, s32[2,2]{1,0:T(2,128)S(1)} %copy-done.2, f32[2,2]{1,0:T(2,128)S(1)} %copy-done.3, s32[2]{0:T(128)S(1)} %copy-done.4, f32[32]{0:T(128)S(1)} %copy-done.5, f32[16,8,128]{2,1,0:T(8,128)S(1)} %all_to_all.16.stats_ref, ...), custom_call_target="tpu_custom_call" | custom-call | flops 805306368 | bytes 6291456 | tf_op jit(solution)/shard_map/gradient_rows/pallas_call | solution.py:194
  52.3 5.8 %all-to-all-start.2 = ((f32[16,128,256]{2,1,0:T(8,128)}), f32[16,128,256]{2,1,0:T(8,128)S(1)}, u32[]{:S(2)}, u32[]{:S(2)}) async-start(f32[16,128,256]{2,1,0:T(8,128)} %get-tuple-element.10), calls=%async_computation.2 | async-start | bytes 4194304 | tf_op jit(solution)/shard_map/all_to_all | solution.py:236
  58.0 15.3 %psum.14 = f32[1,128]{1,0:T(1,128)S(1)} all-reduce(f32[1,128]{1,0:T(1,128)S(1)} %get-tuple-element.11), channel_id=1, replica_groups={{0,16,32,48,64,80,96,112},{1,17,33,49,65,81,97,113},{2,18,34,50,66,82,9..., use_global_device_ids=true, to_apply=%region_1.0 | all-reduce | flops 128 | bytes 1024 | tf_op jit(solution)/shard_map/psum | solution.py:237
  73.3 20.5 %psum.15 = f32[1,128]{1,0:T(1,128)} all-reduce(f32[1,128]{1,0:T(1,128)S(1)} %psum.14), channel_id=1, replica_groups={{0,128,256,384},{1,129,257,385},{2,130,258,386},{3,131,259,387},{4,132,..., use_global_device_ids=true, to_apply=%region_2.0 | all-reduce | flops 128 | bytes 1024 | tf_op jit(solution)/shard_map/psum | solution.py:238
  93.8 0.0 all-to-all-done.2
  93.8 0.8 reduce_sum.9
Async XLA Ops:
  2.2 0.9 copy-start.1
  3.3 33.8 %copy-start = (f32[4096,256]{1,0:T(8,128)S(1)}, f32[4096,256]{1,0:T(8,128)}, u32[]{:S(2)}) copy-start(f32[4096,256]{1,0:T(8,128)} %param.9) | copy-start | bytes 12582916
  37.0 12.2 %copy-start.2 = (s32[2,2]{1,0:T(2,128)S(1)}, s32[2,2]{1,0:T(2,128)}, u32[]{:S(2)}) copy-start(s32[2,2]{1,0:T(2,128)} %lengths_ref.1) | copy-start | bytes 52
  37.0 12.2 %copy-start.3 = (f32[2,2]{1,0:T(2,128)S(1)}, f32[2,2]{1,0:T(2,128)}, u32[]{:S(2)}) copy-start(f32[2,2]{1,0:T(2,128)} %ref_logp_ref.1) | copy-start | bytes 52
  37.0 12.2 %copy-start.4 = (s32[2]{0:T(128)S(1)}, s32[2]{0:T(128)}, u32[]{:S(2)}) copy-start(s32[2]{0:T(128)} %group_map_ref.1) | copy-start | bytes 28
  37.0 12.2 %copy-start.5 = (f32[32]{0:T(128)S(1)}, f32[32]{0:T(128)}, u32[]{:S(2)}) copy-start(f32[32]{0:T(128)} %weight_of_ref.1) | copy-start | bytes 388
  52.3 41.5 %all-to-all-start.2 = ((f32[16,128,256]{2,1,0:T(8,128)}), f32[16,128,256]{2,1,0:T(8,128)S(1)}, u32[]{:S(2)}, u32[]{:S(2)}) async-start(f32[16,128,256]{2,1,0:T(8,128)} %get-tuple-element.10), calls=%async_computation.2 | async-start | bytes 4194304 | tf_op jit(solution)/shard_map/all_to_all | solution.py:236
where the time goes:
time: 94.9 us; the launch traced here: 94.6 us
  blocking collectives  80.3 us (85%)
  starting transfers between devices  5.75 us (6%)
  Pallas kernels  4.58 us (5%)
  local copies, waits for them, and re-layouts  2.46 us (3%)
    all_to_all x1, blocking collectives, shards(): states = lax.all_to_all(state_copies, 'vocab', 0, 0, tiled=True)  33.7 us
    psum x1, blocking collectives, shards(): lax.psum(loss_row, both_axes, axis_index_groups=far_groups(pairs, holders))  20.5 us
    psum x1, blocking collectives, shards(): lax.psum(loss_row, both_axes, axis_index_groups=near_groups(pairs, holders))  15.3 us
    all_to_all x1, blocking collectives, shards(): stats = lax.all_to_all(stat_copies, 'vocab', 0, 0, tiled=True)  10.8 us
    all_to_all x1, starting transfers between devices, shards(): lax.all_to_all(partial_rows, 'vocab', 0, 0, tiled=True)  5.75 us
    pallas_call x1, Pallas kernels, gradient_rows(): pl.pallas_call(rows_kernel, out_shape=(pltpu.HBM(rows_shape, jnp.float32)...  3.05 us
  transfers between devices with their start and end apart: 1, of which 0 were waited for; matrix products, arithmetic and copies ran while one was open for 0% of the time, Pallas kernels for 0%

commit v1 on v0

v1 whole, which is shorter than its diff:
```python
import functools

import jax
import jax.numpy as jnp
from jax import lax
from jax.experimental import pallas as pl
from jax.experimental.pallas import tpu as pltpu
from jax.sharding import PartitionSpec as P

beta_scale = 0.05
both_axes = ("dp", "vocab")
cores = 2
near_chips = 4
stat_rows = 8
vmem_grant = 24 * 1024 * 1024


def chip_plane_groups(pairs, holders):
    return [
        [pair * holders + place for pair in (first, first + 1) for place in range(holders)]
        for first in range(0, pairs, cores)
    ]


def near_groups(pairs, holders):
    block = cores * near_chips
    return [
        [(start + k) * holders + place for k in range(0, block, cores)]
        for first in range(0, pairs, block)
        for start in range(first, first + cores)
        for place in range(holders)
    ]


def far_groups(pairs, holders):
    block = cores * near_chips
    return [
        [(first + k) * holders + place for first in range(0, pairs, block)]
        for k in range(block)
        for place in range(holders)
    ]


def split_parts(values):
    high = values.astype(jnp.bfloat16)
    low = (values - high.astype(jnp.float32)).astype(jnp.bfloat16)
    return high, low


def stacked_parts(values):
    return jnp.concatenate(split_parts(values), axis=0)


def product(both, weight, weight_dim):
    rows = both.shape[0] // 2
    high, low = split_parts(weight)
    dims = (((1,), (weight_dim,)), ((), ()))
    wide = lax.dot_general(both, high, dims, preferred_element_type=jnp.float32)
    narrow = lax.dot_general(both[:rows], low, dims, preferred_element_type=jnp.float32)
    return wide[:rows] + (wide[rows:] + narrow)


def column_matches(target_row, base, columns):
    ids = base + lax.broadcasted_iota(jnp.int32, (columns, target_row.shape[1]), 0)
    return ids == target_row


def copies_kernel(shard_ref, out_ref):
    shard = shard_ref[...]
    for k in range(out_ref.shape[0]):
        out_ref[k] = shard


def copies_for_all(shard, holders):
    return pl.pallas_call(
        copies_kernel,
        out_shape=jax.ShapeDtypeStruct((holders, *shard.shape), shard.dtype),
        in_specs=[pl.BlockSpec(memory_space=pltpu.VMEM)],
        out_specs=pl.BlockSpec(memory_space=pltpu.VMEM),
        compiler_params=pltpu.CompilerParams(vmem_limit_bytes=vmem_grant),
        name="state_copies",
    )(shard)


def token_row(values_ref):
    pairs, ones, _ = values_ref.shape
    pieces = [values_ref[pair, one : one + 1] for pair in range(pairs) for one in range(ones)]
    return jnp.concatenate(pieces, axis=1)


def logits_kernel(
    lengths_ref,
    ref_logp_ref,
    group_map_ref,
    weight_of_ref,
    targets_ref,
    rest_lse_ref,
    states_ref,
    weight_ref,
    scaled_ref,
    matches_ref,
    own_ref,
    stats_ref,
):
    pair_count, _, seq_slots = targets_ref.shape
    target_row = token_row(targets_ref)
    token = lax.broadcasted_iota(jnp.int32, target_row.shape, 1)
    slot, sequence = token % seq_slots, token // seq_slots
    divisor = 0.0
    for k in range(weight_of_ref.shape[0]):
        divisor += weight_of_ref[k]
    divisor = pair_count * divisor
    live = jnp.zeros(target_row.shape, jnp.float32)
    prior = jnp.zeros(target_row.shape, jnp.float32)
    share = jnp.zeros(target_row.shape, jnp.float32)
    for pair in range(pair_count):
        pair_share = weight_of_ref[group_map_ref[pair]]
        for one in range(2):
            here = sequence == 2 * pair + one
            live = jnp.where(here & (slot < lengths_ref[pair, one]), 1.0, live)
            prior = jnp.where(here, ref_logp_ref[pair, one], prior)
            share = jnp.where(here, pair_share, share)
    share = share / divisor

    total = product(stacked_parts(states_ref[0]), weight_ref[0], 0)
    for k in range(1, states_ref.shape[0]):
        total += product(stacked_parts(states_ref[k]), weight_ref[k], 0)
    logits = total.T
    peak = jnp.max(logits, axis=0, keepdims=True)
    scaled = jnp.exp(logits - peak)
    scaled_ref[...] = scaled
    ids = lax.axis_index("vocab") * logits.shape[0] + lax.broadcasted_iota(jnp.int32, logits.shape, 0)
    matches = ids == target_row
    matches_ref[...] = matches.astype(jnp.float32)
    exponentials = jnp.sum(scaled, axis=0, keepdims=True)
    target = jnp.sum(jnp.where(matches, logits, 0.0), axis=0, keepdims=True)
    row = lax.broadcasted_iota(jnp.int32, own_ref.shape, 0)
    stats = jnp.zeros(own_ref.shape, jnp.float32)
    for k, values in enumerate((peak, exponentials, target, token_row(rest_lse_ref), live, prior, share)):
        stats = jnp.where(row == k, values, stats)
    own_ref[...] = stats
    for k in range(stats_ref.shape[0]):
        stats_ref[k] = stats


def local_logits(scalars, targets, rest_lse, states, weight_blocks):
    holders, tokens, _ = states.shape
    columns = weight_blocks.shape[2]
    in_vmem = pl.BlockSpec(memory_space=pltpu.VMEM)
    return pl.pallas_call(
        logits_kernel,
        out_shape=(
            jax.ShapeDtypeStruct((columns, tokens), jnp.float32),
            jax.ShapeDtypeStruct((columns, tokens), jnp.float32),
            jax.ShapeDtypeStruct((stat_rows, tokens), jnp.float32),
            jax.ShapeDtypeStruct((cores * holders, stat_rows, tokens), jnp.float32),
        ),
        in_specs=[pl.BlockSpec(memory_space=pltpu.SMEM)] * len(scalars) + [in_vmem] * 4,
        out_specs=(in_vmem,) * 4,
        compiler_params=pltpu.CompilerParams(vmem_limit_bytes=vmem_grant),
        cost_estimate=pl.CostEstimate(
            flops=6 * states.size * columns,
            bytes_accessed=4 * (states.size + weight_blocks.size),
            transcendentals=tokens * columns,
        ),
        name="local_logits",
    )(*scalars, targets, rest_lse, states, weight_blocks)


def softplus(values):
    small = jnp.exp(-jnp.abs(values))
    shifted = 1.0 + small
    gap = shifted - 1.0
    safe = jnp.where(gap == 0.0, 1.0, gap)
    log_shifted = jnp.where(gap == 0.0, small, jnp.log(shifted) * (small / safe))
    return jnp.maximum(values, 0.0) + log_shifted


def joined(stats):
    peaks, totals, targets = (stats[:, k : k + 1] for k in range(3))
    row_peak = jnp.max(peaks, axis=0)
    row_total = jnp.sum(totals * jnp.exp(peaks - row_peak[None]), axis=0)
    window_lse = row_peak + jnp.log(row_total)
    outside = stats[0, 3:4]
    ceiling = jnp.maximum(window_lse, outside)
    full_lse = ceiling + jnp.log(jnp.exp(window_lse - ceiling) + jnp.exp(outside - ceiling))
    return full_lse, jnp.sum(targets, axis=0)


def preference(full_lse, target_logit, live, prior, share, pair_count):
    tokens = live.shape[1]
    sequence = lax.broadcasted_iota(jnp.int32, live.shape, 1) // (tokens // (2 * pair_count))
    token_logp = live * (target_logit - full_lse)
    token_grad = jnp.zeros(live.shape, jnp.float32)
    loss = jnp.zeros((1, 1), jnp.float32)

    def of_sequence(values, here):
        return jnp.sum(jnp.where(here, values, 0.0), axis=1, keepdims=True)

    def first_of(values, here):
        return jnp.max(jnp.where(here, values, -jnp.inf), axis=1, keepdims=True)

    for pair in range(pair_count):
        chosen, rejected = (sequence == 2 * pair + one for one in range(2))
        margin = beta_scale * (
            (of_sequence(token_logp, chosen) - first_of(prior, chosen))
            - (of_sequence(token_logp, rejected) - first_of(prior, rejected))
        )
        pair_share = first_of(share, chosen)
        loss += pair_share * softplus(-margin)
        coefficient = -beta_scale * pair_share / (1.0 + jnp.exp(margin))
        token_grad += jnp.where(chosen, coefficient, 0.0) - jnp.where(rejected, coefficient, 0.0)
    return loss, live * token_grad


def rows_kernel(
    pair_count, stats_ref, own_ref, scaled_ref, matches_ref, weight_ref, rows_ref, loss_ref, grads_ref, made_ref, sems
):
    holders = weight_ref.shape[0]
    own_core = lax.axis_index("dp") % cores
    mine = pl.ds(pl.multiple_of(own_core * holders, holders), holders)
    full_lse, _ = joined(stats_ref[mine])
    scale = jnp.exp(own_ref[0:1] - full_lse)
    both = stacked_parts((matches_ref[...] - scale * scaled_ref[...]).T)
    sent = []
    for k in range(holders):
        made_ref[k] = product(both, weight_ref[k], 1)
        sent.append(pltpu.make_async_copy(made_ref.at[k], rows_ref.at[k], sems.at[k]))
        sent[k].start()
    loss = jnp.zeros((1, 1), jnp.float32)
    token_grad = jnp.zeros(loss_ref.shape, jnp.float32)
    for core in range(cores):
        stats = stats_ref[pl.ds(core * holders, holders)]
        given = (stats[0, k : k + 1] for k in range(4, 7))
        core_loss, core_grad = preference(*joined(stats), *given, pair_count)
        loss += core_loss
        token_grad = jnp.where(own_core == core, core_grad, token_grad)
    loss_ref[...] = jnp.broadcast_to(loss, loss_ref.shape)
    grads_ref[...] = jnp.broadcast_to(token_grad, grads_ref.shape[::-1]).T
    for copy in sent:
        copy.wait()


def gradient_rows(pair_count, stats, own, scaled, matches, weight_blocks):
    holders, width, columns = weight_blocks.shape
    tokens = own.shape[1]
    rows_shape = (holders, tokens, width)
    in_vmem = pl.BlockSpec(memory_space=pltpu.VMEM)
    return pl.pallas_call(
        functools.partial(rows_kernel, pair_count),
        out_shape=(
            pltpu.HBM(rows_shape, jnp.float32),
            jax.ShapeDtypeStruct((1, tokens), jnp.float32),
            jax.ShapeDtypeStruct((tokens, width), jnp.float32),
        ),
        in_specs=[in_vmem] * 5,
        out_specs=(pl.BlockSpec(memory_space=pltpu.HBM), in_vmem, in_vmem),
        scratch_shapes=[pltpu.VMEM(rows_shape, jnp.float32), pltpu.SemaphoreType.DMA((holders,))],
        compiler_params=pltpu.CompilerParams(vmem_limit_bytes=vmem_grant),
        cost_estimate=pl.CostEstimate(
            flops=6 * tokens * weight_blocks.size,
            bytes_accessed=4 * (holders * tokens * width + weight_blocks.size),
            transcendentals=tokens * holders,
        ),
        name="gradient_rows",
    )(stats, own, scaled, matches, weight_blocks)


def shards(hidden, head_weight, targets, lengths, rest_lse, ref_logp, group_map, group_weight):
    pair_count, _, seq_slots, local_width = hidden.shape
    pairs, holders = lax.axis_size("dp"), lax.axis_size("vocab")
    tokens = pair_count * 2 * seq_slots
    weight_blocks = head_weight.reshape(holders, local_width, -1)

    state_copies = copies_for_all(hidden.reshape(tokens, local_width), holders)
    states = lax.all_to_all(state_copies, "vocab", 0, 0, tiled=True)
    scaled, matches, own_stats, stat_copies = local_logits(
        (lengths, ref_logp, group_map, group_weight), targets, rest_lse, states, weight_blocks
    )
    stats = lax.all_to_all(
        stat_copies, both_axes, 0, 0, axis_index_groups=chip_plane_groups(pairs, holders), tiled=True
    )
    partial_rows, loss_row, token_grads = gradient_rows(
        pair_count, stats, own_stats, scaled, matches, weight_blocks
    )
    summed_rows = jnp.sum(lax.all_to_all(partial_rows, "vocab", 0, 0, tiled=True), axis=0)
    loss_row = lax.psum(loss_row, both_axes, axis_index_groups=near_groups(pairs, holders))
    loss_row = lax.psum(loss_row, both_axes, axis_index_groups=far_groups(pairs, holders))
    return ((token_grads * summed_rows).reshape(hidden.shape), loss_row[0, 0])


def solution(mesh):
    return jax.shard_map(
        shards,
        mesh=mesh,
        in_specs=(
            P("dp", None, None, "vocab"),
            P(None, "vocab"),
            P("dp", None, None),
            P("dp", None),
            P("dp", None, None),
            P("dp", None),
            P("dp"),
            P(),
        ),
        out_specs=(P("dp", None, None, "vocab"), P()),
        check_vma=False,
    )
```

time: 94.9 us -> 91.4 us (0.963)
  the two profiles are of different devices: /device:TPU:4 before, /device:TPU:1 now
where the time goes in v1:
time: 91.4 us; the launch traced here: 91.2 us
  blocking collectives  75.8 us (83%)
  Pallas kernels  4.63 us (5%)
  waiting for transfers between devices  4.5 us (5%)
  starting transfers between devices  3.73 us (4%)
  local copies, waits for them, and re-layouts  0.93 us (1%)
    all_to_all x1, blocking collectives, shards(): states = lax.all_to_all(state_copies, 'vocab', 0, 0, tiled=True)  34.7 us
    psum x1, blocking collectives, shards(): lax.psum(loss_row, both_axes, axis_index_groups=far_groups(pairs, holders))  17.1 us
    all_to_all x1, blocking collectives, shards(): lax.all_to_all(stat_copies, both_axes, 0, 0, axis_index_groups=chip_plane...  13 us
    psum x1, blocking collectives, shards(): lax.psum(loss_row, both_axes, axis_index_groups=near_groups(pairs, holders))  11 us
    all_to_all x1, waiting for transfers between devices, shards(): lax.all_to_all(partial_rows, 'vocab', 0, 0, tiled=True)  4.5 us
    all_to_all x1, starting transfers between devices, shards(): lax.all_to_all(partial_rows, 'vocab', 0, 0, tiled=True)  3.73 us
    pallas_call x1, Pallas kernels, gradient_rows(): pl.pallas_call(functools.partial(rows_kernel, pair_count), out_shape=(plt...  2.44 us
    pallas_call x1, Pallas kernels, local_logits(): pl.pallas_call(logits_kernel, out_shape=(jax.ShapeDtypeStruct((columns, t...  1.99 us
  transfers between devices with their start and end apart: 1, of which 1 were waited for; matrix products, arithmetic and copies ran while one was open for 0% of the time, Pallas kernels for 0%

profile of v1, /device:TPU:1, one launch (start us, length us, event | category | flops | bytes accessed | tf_op | source)
XLA Modules:
  0.0 91.2 jit_solution(16251224589782775128)
XLA Ops:
  0.6 0.0 copy-start.1
  0.6 0.9 copy-done.1
  1.5 0.0 copy-start.2
  1.5 0.0 copy-start.3
  1.5 0.0 copy-start.5
  1.5 0.0 copy-start.7
  1.5 0.2 state_copies.1
  1.8 0.0 copy-start
  1.8 0.0 copy-start.4
  1.8 0.0 copy-start.6
  1.8 34.7 %all_to_all.15.states_ref = f32[16,128,256]{2,1,0:T(8,128)S(1)} all-to-all(f32[16,128,256]{2,1,0:T(8,128)S(1)} %state_copies.1), channel_id=1, replica_groups=mesh['dp'=32,'vocab'=16] {'vocab'}, dimensions={0} | all-to-all | bytes 4194304 | tf_op jit(solution)/shard_map/all_to_all | solution.py:276
  36.5 0.0 copy-done.2
  36.5 0.0 copy-done.3
  36.5 0.0 copy-done.5
  36.5 0.0 copy-done.7
  36.5 0.0 copy-done
  36.5 0.0 copy-done.4
  36.5 0.0 copy-done.6
  36.5 2.0 %local_logits.1 = (f32[256,128]{1,0:T(8,128)S(1)}, f32[256,128]{1,0:T(8,128)S(1)}, f32[8,128]{1,0:T(8,128)S(1)}, f32[32,8,128]{2,1,0:T(8,128)S(1)}) custom-call(s32[2,2]{1,0:T(2,128)S(1)} %copy-done.4, f32[2,2]{1,0:T(2,128)S(1)} %copy-done.5, s32[2]{0:T(128)S(1)} %copy-done.6, f32[32]{0:T(128)S(1)} %copy-done.7, s32[2,2,32]{2,1,0:T(2,128)S(1)} %copy-done.2, ...), custom_call_target="tpu_custom_call" | custom-call | flops 805306368 | bytes 6291456 | tf_op jit(solution)/shard_map/local_logits/pallas_call | solution.py:150
  38.5 13.0 %all_to_all.16.stats_ref = f32[32,8,128]{2,1,0:T(8,128)S(1)} all-to-all(f32[32,8,128]{2,1,0:T(8,128)S(1)} %get-tuple-element.9), channel_id=1, replica_groups={{0,1,2,3,4,5,6,7,8,9,10,11,12,13,14,15,16,17,18,19,20,21,22,23,24,25,26..., dimensions={0} | all-to-all | bytes 262144 | tf_op jit(solution)/shard_map/all_to_all | solution.py:280
  51.6 2.4 %gradient_rows.1 = (f32[16,128,256]{2,1,0:T(8,128)}, f32[1,128]{1,0:T(1,128)S(1)}, f32[128,256]{1,0:T(8,128)S(1)}) custom-call(f32[32,8,128]{2,1,0:T(8,128)S(1)} %all_to_all.16.stats_ref, f32[8,128]{1,0:T(8,128)S(1)} %get-tuple-element.10.own_ref, f32[256,128]{1,0:T(8,128)S(1)} %get-tuple-element.11.scaled_ref, ...), custom_call_target="tpu_custom_call" | custom-call | flops 805306368 | bytes 6291456 | tf_op jit(solution)/shard_map/gradient_rows/pallas_call | solution.py:249
  54.0 3.7 %all-to-all-start.2 = ((f32[16,128,256]{2,1,0:T(8,128)}), f32[16,128,256]{2,1,0:T(8,128)S(1)}, u32[]{:S(2)}, u32[]{:S(2)}) async-start(f32[16,128,256]{2,1,0:T(8,128)} %get-tuple-element.14), calls=%async_computation.2 | async-start | bytes 4194304 | tf_op jit(solution)/shard_map/all_to_all | solution.py:286
  57.8 11.0 %psum.14 = f32[1,128]{1,0:T(1,128)S(1)} all-reduce(f32[1,128]{1,0:T(1,128)S(1)} %get-tuple-element.15), channel_id=1, replica_groups={{0,32,64,96},{1,33,65,97},{2,34,66,98},{3,35,67,99},{4,36,68,100},{5,37..., use_global_device_ids=true, to_apply=%region_1.0 | all-reduce | flops 128 | bytes 1024 | tf_op jit(solution)/shard_map/psum | solution.py:287
  68.8 17.1 %psum.15 = f32[1,128]{1,0:T(1,128)} all-reduce(f32[1,128]{1,0:T(1,128)S(1)} %psum.14), channel_id=1, replica_groups={{0,128,256,384},{1,129,257,385},{2,130,258,386},{3,131,259,387},{4,132,..., use_global_device_ids=true, to_apply=%region_2.0 | all-reduce | flops 128 | bytes 1024 | tf_op jit(solution)/shard_map/psum | solution.py:288
  85.9 4.5 %all-to-all-done.2 = f32[16,128,256]{2,1,0:T(8,128)S(1)} async-done(((f32[16,128,256]{2,1,0:T(8,128)}), f32[16,128,256]{2,1,0:T(8,128)S(1)}, u32[]{:S(2)}, u32[]{:S(2)}) %all-to-all-start.2) | async-done | bytes 2097184 | tf_op jit(solution)/shard_map/all_to_all | solution.py:286
  90.3 0.1 reduce_sum.9
  90.5 0.7 mul.3
Async XLA Ops:
  0.6 0.9 copy-start.1
  1.5 35.0 %copy-start.2 = (s32[2,2,32]{2,1,0:T(2,128)S(1)}, s32[2,2,32]{2,1,0:T(2,128)}, u32[]{:S(2)}) copy-start(s32[2,2,32]{2,1,0:T(2,128)} %targets_ref.1) | copy-start | bytes 1540
  1.5 35.0 %copy-start.3 = (f32[2,2,32]{2,1,0:T(2,128)S(1)}, f32[2,2,32]{2,1,0:T(2,128)}, u32[]{:S(2)}) copy-start(f32[2,2,32]{2,1,0:T(2,128)} %rest_lse_ref.1) | copy-start | bytes 1540
  1.5 35.0 %copy-start.5 = (f32[2,2]{1,0:T(2,128)S(1)}, f32[2,2]{1,0:T(2,128)}, u32[]{:S(2)}) copy-start(f32[2,2]{1,0:T(2,128)} %ref_logp_ref.1) | copy-start | bytes 52
  1.5 35.0 %copy-start.7 = (f32[32]{0:T(128)S(1)}, f32[32]{0:T(128)}, u32[]{:S(2)}) copy-start(f32[32]{0:T(128)} %weight_of_ref.1) | copy-start | bytes 388
  1.8 34.8 %copy-start = (f32[4096,256]{1,0:T(8,128)S(1)}, f32[4096,256]{1,0:T(8,128)}, u32[]{:S(2)}) copy-start(f32[4096,256]{1,0:T(8,128)} %param.9) | copy-start | bytes 12582916
  1.8 34.8 %copy-start.4 = (s32[2,2]{1,0:T(2,128)S(1)}, s32[2,2]{1,0:T(2,128)}, u32[]{:S(2)}) copy-start(s32[2,2]{1,0:T(2,128)} %lengths_ref.1) | copy-start | bytes 52
  1.8 34.8 %copy-start.6 = (s32[2]{0:T(128)S(1)}, s32[2]{0:T(128)}, u32[]{:S(2)}) copy-start(s32[2]{0:T(128)} %group_map_ref.1) | copy-start | bytes 28
  54.0 36.3 %all-to-all-start.2 = ((f32[16,128,256]{2,1,0:T(8,128)}), f32[16,128,256]{2,1,0:T(8,128)S(1)}, u32[]{:S(2)}, u32[]{:S(2)}) async-start(f32[16,128,256]{2,1,0:T(8,128)} %get-tuple-element.14), calls=%async_computation.2 | async-start | bytes 4194304 | tf_op jit(solution)/shard_map/all_to_all | solution.py:286

commit v2 on v1

--- a/solution.py
+++ b/solution.py
@@ -10,9 +10,20 @@
 beta_scale = 0.05
 both_axes = ("dp", "vocab")
 cores = 2
+side = 4
 near_chips = 4
 stat_rows = 8
 vmem_grant = 24 * 1024 * 1024
+
+
+def line_groups(pairs, holders, first):
+    groups = []
+    for pair in range(pairs):
+        along_x = (pair % cores == 0) == first
+        for line in range(side):
+            places = [line * side + k if along_x else k * side + line for k in range(side)]
+            groups.append([pair * holders + place for place in places])
+    return groups
 
 
 def chip_plane_groups(pairs, holders):
@@ -63,6 +74,10 @@
 def column_matches(target_row, base, columns):
     ids = base + lax.broadcasted_iota(jnp.int32, (columns, target_row.shape[1]), 0)
     return ids == target_row
+
+
+def holder_of(block, own_core):
+    return jnp.where(own_core == 0, block, (block % side) * side + block // side)
 
 
 def copies_kernel(shard_ref, out_ref):
@@ -122,9 +137,10 @@
             share = jnp.where(here, pair_share, share)
     share = share / divisor
 
+    own_core = lax.axis_index("dp") % cores
     total = product(stacked_parts(states_ref[0]), weight_ref[0], 0)
     for k in range(1, states_ref.shape[0]):
-        total += product(stacked_parts(states_ref[k]), weight_ref[k], 0)
+        total += product(stacked_parts(states_ref[k]), weight_ref[holder_of(k, own_core)], 0)
     logits = total.T
     peak = jnp.max(logits, axis=0, keepdims=True)
     scaled = jnp.exp(logits - peak)
@@ -224,7 +240,7 @@
     both = stacked_parts((matches_ref[...] - scale * scaled_ref[...]).T)
     sent = []
     for k in range(holders):
-        made_ref[k] = product(both, weight_ref[k], 1)
+        made_ref[k] = product(both, weight_ref[holder_of(k, own_core)], 1)
         sent.append(pltpu.make_async_copy(made_ref.at[k], rows_ref.at[k], sems.at[k]))
         sent[k].start()
     loss = jnp.zeros((1, 1), jnp.float32)
@@ -266,26 +282,64 @@
     )(stats, own, scaled, matches, weight_blocks)
 
 
+def line_sum_kernel(parts_ref, loss_ref, sums_ref, passed_ref, made_ref, sems):
+    passed_ref[...] = loss_ref[...]
+    sent = []
+    for k in range(made_ref.shape[0]):
+        made_ref[k] = jnp.sum(parts_ref[:, k], axis=0)
+        sent.append(pltpu.make_async_copy(made_ref.at[k], sums_ref.at[k], sems.at[k]))
+        sent[k].start()
+    for copy in sent:
+        copy.wait()
+
+
+def line_sums(parts, loss_row):
+    shape = parts.shape[1:]
+    in_vmem = pl.BlockSpec(memory_space=pltpu.VMEM)
+    return pl.pallas_call(
+        line_sum_kernel,
+        out_shape=(
+            pltpu.HBM(shape, jnp.float32),
+            jax.ShapeDtypeStruct(loss_row.shape, jnp.float32),
+        ),
+        in_specs=[in_vmem] * 2,
+        out_specs=(pl.BlockSpec(memory_space=pltpu.HBM), in_vmem),
+        scratch_shapes=[pltpu.VMEM(shape, jnp.float32), pltpu.SemaphoreType.DMA((shape[0],))],
+        compiler_params=pltpu.CompilerParams(vmem_limit_bytes=vmem_grant),
+        name="line_sums",
+    )(parts, loss_row)
+
+
+def exchanged(blocks, groups):
+    return lax.all_to_all(blocks, both_axes, 0, 0, axis_index_groups=groups, tiled=True)
+
+
 def shards(hidden, head_weight, targets, lengths, rest_lse, ref_logp, group_map, group_weight):
     pair_count, _, seq_slots, local_width = hidden.shape
     pairs, holders = lax.axis_size("dp"), lax.axis_size("vocab")
     tokens = pair_count * 2 * seq_slots
     weight_blocks = head_weight.reshape(holders, local_width, -1)
 
-    state_copies = copies_for_all(hidden.reshape(tokens, local_width), holders)
-    states = lax.all_to_all(state_copies, "vocab", 0, 0, tiled=True)
+    first_lines = line_groups(pairs, holders, True)
+    second_lines = line_groups(pairs, holders, False)
+
+    near = exchanged(copies_for_all(hidden.reshape(tokens, local_width), side), first_lines)
+    states = exchanged(jnp.broadcast_to(near, (side, *near.shape)), second_lines)
+    states = states.reshape(holders, tokens, local_width)
     scaled, matches, own_stats, stat_copies = local_logits(
         (lengths, ref_logp, group_map, group_weight), targets, rest_lse, states, weight_blocks
     )
-    stats = lax.all_to_all(
-        stat_copies, both_axes, 0, 0, axis_index_groups=chip_plane_groups(pairs, holders), tiled=True
-    )
+    stats = exchanged(stat_copies, chip_plane_groups(pairs, holders))
     partial_rows, loss_row, token_grads = gradient_rows(
         pair_count, stats, own_stats, scaled, matches, weight_blocks
     )
-    summed_rows = jnp.sum(lax.all_to_all(partial_rows, "vocab", 0, 0, tiled=True), axis=0)
+    line_parts = exchanged(
+        partial_rows.reshape(side, side, tokens, local_width), second_lines
+    )
+    loss_row = lax.psum(loss_row, both_axes, axis_index_groups=far_groups(pairs, holders))
+    line_rows, loss_row = line_sums(line_parts, loss_row)
+    summed_rows = jnp.sum(exchanged(line_rows, first_lines), axis=0)
     loss_row = lax.psum(loss_row, both_axes, axis_index_groups=near_groups(pairs, holders))
-    loss_row = lax.psum(loss_row, both_axes, axis_index_groups=far_groups(pairs, holders))
     return ((token_grads * summed_rows).reshape(hidden.shape), loss_row[0, 0])
 
 

time: 91.4 us -> 92.4 us (1.011)
  the two profiles are of different devices: /device:TPU:1 before, /device:TPU:10 now
where the time goes in v2:
time: 92.4 us; the launch traced here: 92 us
  blocking collectives  74.3 us (80%)
  starting transfers between devices  9.95 us (11%)
  Pallas kernels  5.11 us (6%)
  local copies, waits for them, and re-layouts  1.13 us (1%)
    all_to_all x3, blocking collectives, exchanged(): lax.all_to_all(blocks, both_axes, 0, 0, axis_index_groups=groups, tiled=T...  44.2 us
    psum x1, blocking collectives, shards(): lax.psum(loss_row, both_axes, axis_index_groups=far_groups(pairs, holders))  19.4 us
    psum x1, blocking collectives, shards(): lax.psum(loss_row, both_axes, axis_index_groups=near_groups(pairs, holders))  10.8 us
    all_to_all x2, starting transfers between devices, exchanged(): lax.all_to_all(blocks, both_axes, 0, 0, axis_index_groups=groups, tiled=T...  9.95 us
    pallas_call x1, Pallas kernels, gradient_rows(): pl.pallas_call(functools.partial(rows_kernel, pair_count), out_shape=(plt...  2.4 us
  transfers between devices with their start and end apart: 2, of which 0 were waited for; matrix products, arithmetic and copies ran while one was open for 0% of the time, Pallas kernels for 0%

profile of v2, /device:TPU:10, one launch (start us, length us, event | category | flops | bytes accessed | tf_op | source)
XLA Modules:
  0.0 92.0 jit_solution(18126352431404813305)
XLA Ops:
  0.6 0.0 copy-start.1
  0.6 0.9 copy-done.1
  1.6 11.3 %all_to_all.25 = f32[4,128,256]{2,1,0:T(8,128)S(1)} all-to-all(f32[4,128,256]{2,1,0:T(8,128)S(1)} %state_copies.1), channel_id=1, replica_groups={{0,1,2,3},{4,5,6,7},{8,9,10,11},{12,13,14,15},{16,20,24,28},{17,21,25,2..., dimensions={0} | all-to-all | bytes 1048576 | tf_op jit(solution)/shard_map/all_to_all | solution.py:314
  12.8 0.0 copy-start.3
  12.8 0.0 copy-start.5
  12.8 0.0 copy-start.7
  12.8 0.2 broadcast_in_dim.3
  13.0 0.0 copy-start
  13.0 0.0 copy-start.2
  13.1 0.0 copy-start.4
  13.1 0.0 copy-start.6
  13.1 21.9 %all_to_all.26 = f32[4,4,128,256]{3,2,1,0:T(8,128)S(1)} all-to-all(f32[4,4,128,256]{3,2,1,0:T(8,128)S(1)} %broadcast_in_dim.3), channel_id=1, replica_groups={{0,4,8,12},{1,5,9,13},{2,6,10,14},{3,7,11,15},{16,17,18,19},{20,21,22,2..., dimensions={0} | all-to-all | bytes 4194304 | tf_op jit(solution)/shard_map/all_to_all | solution.py:314
  35.0 0.0 copy-done.3
  35.0 0.0 copy-done.5
  35.0 0.0 copy-done.7
  35.0 0.0 copy-done
  35.0 0.0 copy-done.2
  35.0 0.0 copy-done.4
  35.0 0.0 copy-done.6
  35.0 1.8 %local_logits.1 = (f32[256,128]{1,0:T(8,128)S(1)}, f32[256,128]{1,0:T(8,128)S(1)}, f32[8,128]{1,0:T(8,128)S(1)}, f32[32,8,128]{2,1,0:T(8,128)S(1)}) custom-call(s32[2,2]{1,0:T(2,128)S(1)} %copy-done.4, f32[2,2]{1,0:T(2,128)S(1)} %copy-done.5, s32[2]{0:T(128)S(1)} %copy-done.6, f32[32]{0:T(128)S(1)} %copy-done.7, s32[2,2,32]{2,1,0:T(2,128)S(1)} %copy-done.2, ...), custom_call_target="tpu_custom_call" | custom-call | flops 805306368 | bytes 6291456 | tf_op jit(solution)/shard_map/local_logits/pallas_call | solution.py:166
  36.8 11.0 %all_to_all.27.stats_ref = f32[32,8,128]{2,1,0:T(8,128)S(1)} all-to-all(f32[32,8,128]{2,1,0:T(8,128)S(1)} %get-tuple-element.11), channel_id=1, replica_groups={{0,1,2,3,4,5,6,7,8,9,10,11,12,13,14,15,16,17,18,19,20,21,22,23,24,25,26..., dimensions={0} | all-to-all | bytes 262144 | tf_op jit(solution)/shard_map/all_to_all | solution.py:314
  47.9 2.4 %gradient_rows.1 = (f32[16,128,256]{2,1,0:T(8,128)}, f32[1,128]{1,0:T(1,128)S(1)}, f32[128,256]{1,0:T(8,128)S(1)}) custom-call(f32[32,8,128]{2,1,0:T(8,128)S(1)} %all_to_all.27.stats_ref, f32[8,128]{1,0:T(8,128)S(1)} %get-tuple-element.12.own_ref, f32[256,128]{1,0:T(8,128)S(1)} %get-tuple-element.13.scaled_ref, ...), custom_call_target="tpu_custom_call" | custom-call | flops 805306368 | bytes 6291456 | tf_op jit(solution)/shard_map/gradient_rows/pallas_call | solution.py:265
  50.3 5.1 %all-to-all-start.3 = ((f32[4,4,128,256]{3,2,1,0:T(8,128)}), f32[4,4,128,256]{3,2,1,0:T(8,128)S(1)}, u32[]{:S(2)}, u32[]{:S(2)}) async-start(f32[4,4,128,256]{3,2,1,0:T(8,128)} %bitcast.11), calls=%async_computation.3 | async-start | bytes 4194304 | tf_op jit(solution)/shard_map/all_to_all | solution.py:314
  55.4 19.4 %psum.14.loss_ref = f32[1,128]{1,0:T(1,128)S(1)} all-reduce(f32[1,128]{1,0:T(1,128)S(1)} %get-tuple-element.17), channel_id=1, replica_groups={{0,128,256,384},{1,129,257,385},{2,130,258,386},{3,131,259,387},{4,132,..., use_global_device_ids=true, to_apply=%region_0.0 | all-reduce | flops 128 | bytes 1024 | tf_op jit(solution)/shard_map/psum | solution.py:339
  74.8 0.0 all-to-all-done.3.parts_ref
  74.8 0.9 line_sums.1
  75.6 4.9 %all-to-all-start.4 = ((f32[4,128,256]{2,1,0:T(8,128)}), f32[4,128,256]{2,1,0:T(8,128)S(1)}, u32[]{:S(2)}, u32[]{:S(2)}) async-start(f32[4,128,256]{2,1,0:T(8,128)} %get-tuple-element.18), calls=%async_computation.4 | async-start | bytes 1048576 | tf_op jit(solution)/shard_map/all_to_all | solution.py:314
  80.5 10.8 %psum.15 = f32[1,128]{1,0:T(1,128)} all-reduce(f32[1,128]{1,0:T(1,128)S(1)} %get-tuple-element.19), channel_id=1, replica_groups={{0,32,64,96},{1,33,65,97},{2,34,66,98},{3,35,67,99},{4,36,68,100},{5,37..., use_global_device_ids=true, to_apply=%region_2.0 | all-reduce | flops 128 | bytes 1024 | tf_op jit(solution)/shard_map/psum | solution.py:342
  91.3 0.0 all-to-all-done.4
  91.3 0.7 mul.3
  (2 shorter events, 0.1 us)
Async XLA Ops:
  0.6 0.9 copy-start.1
  12.8 22.1 %copy-start.3 = (f32[2,2,32]{2,1,0:T(2,128)S(1)}, f32[2,2,32]{2,1,0:T(2,128)}, u32[]{:S(2)}) copy-start(f32[2,2,32]{2,1,0:T(2,128)} %rest_lse_ref.1) | copy-start | bytes 1540
  12.8 22.1 %copy-start.5 = (f32[2,2]{1,0:T(2,128)S(1)}, f32[2,2]{1,0:T(2,128)}, u32[]{:S(2)}) copy-start(f32[2,2]{1,0:T(2,128)} %ref_logp_ref.1) | copy-start | bytes 52
  12.8 22.1 %copy-start.7 = (f32[32]{0:T(128)S(1)}, f32[32]{0:T(128)}, u32[]{:S(2)}) copy-start(f32[32]{0:T(128)} %weight_of_ref.1) | copy-start | bytes 388
  13.0 21.9 %copy-start = (f32[4096,256]{1,0:T(8,128)S(1)}, f32[4096,256]{1,0:T(8,128)}, u32[]{:S(2)}) copy-start(f32[4096,256]{1,0:T(8,128)} %param.9) | copy-start | bytes 12582916
  13.0 21.9 %copy-start.2 = (s32[2,2,32]{2,1,0:T(2,128)S(1)}, s32[2,2,32]{2,1,0:T(2,128)}, u32[]{:S(2)}) copy-start(s32[2,2,32]{2,1,0:T(2,128)} %targets_ref.1) | copy-start | bytes 1540
  13.1 21.9 %copy-start.4 = (s32[2,2]{1,0:T(2,128)S(1)}, s32[2,2]{1,0:T(2,128)}, u32[]{:S(2)}) copy-start(s32[2,2]{1,0:T(2,128)} %lengths_ref.1) | copy-start | bytes 52
  13.1 21.9 %copy-start.6 = (s32[2]{0:T(128)S(1)}, s32[2]{0:T(128)}, u32[]{:S(2)}) copy-start(s32[2]{0:T(128)} %group_map_ref.1) | copy-start | bytes 28
  50.3 24.5 %all-to-all-start.3 = ((f32[4,4,128,256]{3,2,1,0:T(8,128)}), f32[4,4,128,256]{3,2,1,0:T(8,128)S(1)}, u32[]{:S(2)}, u32[]{:S(2)}) async-start(f32[4,4,128,256]{3,2,1,0:T(8,128)} %bitcast.11), calls=%async_computation.3 | async-start | bytes 4194304 | tf_op jit(solution)/shard_map/all_to_all | solution.py:314
  75.6 15.7 %all-to-all-start.4 = ((f32[4,128,256]{2,1,0:T(8,128)}), f32[4,128,256]{2,1,0:T(8,128)S(1)}, u32[]{:S(2)}, u32[]{:S(2)}) async-start(f32[4,128,256]{2,1,0:T(8,128)} %get-tuple-element.18), calls=%async_computation.4 | async-start | bytes 1048576 | tf_op jit(solution)/shard_map/all_to_all | solution.py:314

commit v3 on v2

--- a/solution.py
+++ b/solution.py
@@ -282,8 +282,8 @@
     )(stats, own, scaled, matches, weight_blocks)
 
 
-def line_sum_kernel(parts_ref, loss_ref, sums_ref, passed_ref, made_ref, sems):
-    passed_ref[...] = loss_ref[...]
+def line_sum_kernel(parts_ref, losses_ref, sums_ref, loss_ref, made_ref, sems):
+    loss_ref[...] = jnp.sum(losses_ref[...], axis=0, keepdims=True)
     sent = []
     for k in range(made_ref.shape[0]):
         made_ref[k] = jnp.sum(parts_ref[:, k], axis=0)
@@ -293,25 +293,29 @@
         copy.wait()
 
 
-def line_sums(parts, loss_row):
+def line_sums(parts, loss_rows):
     shape = parts.shape[1:]
     in_vmem = pl.BlockSpec(memory_space=pltpu.VMEM)
     return pl.pallas_call(
         line_sum_kernel,
         out_shape=(
             pltpu.HBM(shape, jnp.float32),
-            jax.ShapeDtypeStruct(loss_row.shape, jnp.float32),
+            jax.ShapeDtypeStruct((1, loss_rows.shape[1]), jnp.float32),
         ),
         in_specs=[in_vmem] * 2,
         out_specs=(pl.BlockSpec(memory_space=pltpu.HBM), in_vmem),
         scratch_shapes=[pltpu.VMEM(shape, jnp.float32), pltpu.SemaphoreType.DMA((shape[0],))],
         compiler_params=pltpu.CompilerParams(vmem_limit_bytes=vmem_grant),
         name="line_sums",
-    )(parts, loss_row)
+    )(parts, loss_rows)
 
 
 def exchanged(blocks, groups):
     return lax.all_to_all(blocks, both_axes, 0, 0, axis_index_groups=groups, tiled=True)
+
+
+def gathered(row, groups):
+    return lax.all_gather(row, both_axes, axis_index_groups=groups, axis=0, tiled=True)
 
 
 def shards(hidden, head_weight, targets, lengths, rest_lse, ref_logp, group_map, group_weight):
@@ -336,11 +340,12 @@
     line_parts = exchanged(
         partial_rows.reshape(side, side, tokens, local_width), second_lines
     )
-    loss_row = lax.psum(loss_row, both_axes, axis_index_groups=far_groups(pairs, holders))
-    line_rows, loss_row = line_sums(line_parts, loss_row)
+    far_rows = gathered(loss_row, far_groups(pairs, holders))
+    line_rows, loss_row = line_sums(line_parts, far_rows)
     summed_rows = jnp.sum(exchanged(line_rows, first_lines), axis=0)
-    loss_row = lax.psum(loss_row, both_axes, axis_index_groups=near_groups(pairs, holders))
-    return ((token_grads * summed_rows).reshape(hidden.shape), loss_row[0, 0])
+    near_rows = gathered(loss_row, near_groups(pairs, holders))
+    dpo_loss = jnp.sum(near_rows, axis=0)[0]
+    return ((token_grads * summed_rows).reshape(hidden.shape), dpo_loss)
 
 
 def solution(mesh):

time: 92.4 us -> 91 us (0.985)
  blocking collectives: 74.3 us -> 72.3 us
    psum x2 -> x0, blocking collectives: 30.2 us -> none  [the longest x1 19.4 us: shards(): lax.psum(loss_row, both_axes, axis_index_groups=far_groups(pairs, holders))]
    all_gather x0 -> x2, blocking collectives: none -> 28.1 us  [gathered(): lax.all_gather(row, both_axes, axis_index_groups=groups, axis=0, tiled=True)]
  transfers between devices with their start and end apart: 2 -> 2, of which waited for: 0 -> 0; matrix products, arithmetic and copies ran while one was open for 0% -> 1% of each run, Pallas kernels for 0% -> 0%
where the time goes in v3:
time: 91 us; the launch traced here: 90.6 us
  blocking collectives  72.3 us (79%)
  starting transfers between devices  9.97 us (11%)
  Pallas kernels  5.24 us (6%)
  other arithmetic  1.24 us (1%)
  local copies, waits for them, and re-layouts  1.13 us (1%)
    all_to_all x3, blocking collectives, exchanged(): lax.all_to_all(blocks, both_axes, 0, 0, axis_index_groups=groups, tiled=T...  44.2 us
    all_gather x2, blocking collectives, gathered(): lax.all_gather(row, both_axes, axis_index_groups=groups, axis=0, tiled=True)  28.1 us
    all_to_all x2, starting transfers between devices, exchanged(): lax.all_to_all(blocks, both_axes, 0, 0, axis_index_groups=groups, tiled=T...  9.97 us
    pallas_call x1, Pallas kernels, gradient_rows(): pl.pallas_call(functools.partial(rows_kernel, pair_count), out_shape=(plt...  2.4 us
    pallas_call x1, Pallas kernels, local_logits(): pl.pallas_call(logits_kernel, out_shape=(jax.ShapeDtypeStruct((columns, t...  1.94 us
  transfers between devices with their start and end apart: 2, of which 0 were waited for; matrix products, arithmetic and copies ran while one was open for 1% of the time, Pallas kernels for 0%

profile of v3, /device:TPU:10, one launch (start us, length us, event | category | flops | bytes accessed | tf_op | source)
XLA Modules:
  0.0 90.6 jit_solution(2159037087091496434)
XLA Ops:
  0.6 0.0 copy-start.1
  0.6 0.9 copy-done.1
  1.6 11.3 %all_to_all.25 = f32[4,128,256]{2,1,0:T(8,128)S(1)} all-to-all(f32[4,128,256]{2,1,0:T(8,128)S(1)} %state_copies.1), channel_id=1, replica_groups={{0,1,2,3},{4,5,6,7},{8,9,10,11},{12,13,14,15},{16,20,24,28},{17,21,25,2..., dimensions={0} | all-to-all | bytes 1048576 | tf_op jit(solution)/shard_map/all_to_all | solution.py:314
  12.8 0.0 copy-start.3
  12.8 0.0 copy-start.5
  12.8 0.0 copy-start.7
  12.8 0.2 broadcast_in_dim.3
  13.0 0.0 copy-start
  13.0 0.0 copy-start.2
  13.1 0.0 copy-start.4
  13.1 0.0 copy-start.6
  13.1 21.9 %all_to_all.26 = f32[4,4,128,256]{3,2,1,0:T(8,128)S(1)} all-to-all(f32[4,4,128,256]{3,2,1,0:T(8,128)S(1)} %broadcast_in_dim.3), channel_id=1, replica_groups={{0,4,8,12},{1,5,9,13},{2,6,10,14},{3,7,11,15},{16,17,18,19},{20,21,22,2..., dimensions={0} | all-to-all | bytes 4194304 | tf_op jit(solution)/shard_map/all_to_all | solution.py:314
  35.0 0.0 copy-done.3
  35.0 0.0 copy-done.5
  35.0 0.0 copy-done.7
  35.0 0.0 copy-done
  35.0 0.0 copy-done.2
  35.0 0.0 copy-done.4
  35.0 0.0 copy-done.6
  35.0 1.9 %local_logits.1 = (f32[256,128]{1,0:T(8,128)S(1)}, f32[256,128]{1,0:T(8,128)S(1)}, f32[8,128]{1,0:T(8,128)S(1)}, f32[32,8,128]{2,1,0:T(8,128)S(1)}) custom-call(s32[2,2]{1,0:T(2,128)S(1)} %copy-done.4, f32[2,2]{1,0:T(2,128)S(1)} %copy-done.5, s32[2]{0:T(128)S(1)} %copy-done.6, f32[32]{0:T(128)S(1)} %copy-done.7, s32[2,2,32]{2,1,0:T(2,128)S(1)} %copy-done.2, ...), custom_call_target="tpu_custom_call" | custom-call | flops 805306368 | bytes 6291456 | tf_op jit(solution)/shard_map/local_logits/pallas_call | solution.py:166
  37.0 11.0 %all_to_all.27.stats_ref = f32[32,8,128]{2,1,0:T(8,128)S(1)} all-to-all(f32[32,8,128]{2,1,0:T(8,128)S(1)} %get-tuple-element.11), channel_id=1, replica_groups={{0,1,2,3,4,5,6,7,8,9,10,11,12,13,14,15,16,17,18,19,20,21,22,23,24,25,26..., dimensions={0} | all-to-all | bytes 262144 | tf_op jit(solution)/shard_map/all_to_all | solution.py:314
  48.0 2.4 %gradient_rows.1 = (f32[16,128,256]{2,1,0:T(8,128)}, f32[1,128]{1,0:T(1,128)S(1)}, f32[128,256]{1,0:T(8,128)S(1)}) custom-call(f32[32,8,128]{2,1,0:T(8,128)S(1)} %all_to_all.27.stats_ref, f32[8,128]{1,0:T(8,128)S(1)} %get-tuple-element.12.own_ref, f32[256,128]{1,0:T(8,128)S(1)} %get-tuple-element.13.scaled_ref, ...), custom_call_target="tpu_custom_call" | custom-call | flops 805306368 | bytes 6291456 | tf_op jit(solution)/shard_map/gradient_rows/pallas_call | solution.py:265
  50.4 5.1 %all-to-all-start.3 = ((f32[4,4,128,256]{3,2,1,0:T(8,128)}), f32[4,4,128,256]{3,2,1,0:T(8,128)S(1)}, u32[]{:S(2)}, u32[]{:S(2)}) async-start(f32[4,4,128,256]{3,2,1,0:T(8,128)} %bitcast.17), calls=%async_computation.3 | async-start | bytes 4194304 | tf_op jit(solution)/shard_map/all_to_all | solution.py:314
  55.5 18.6 %all-gather = f32[4,1,128]{2,1,0:T(1,128)S(1)} all-gather(f32[1,1,128]{2,1,0:T(1,128)S(1)} %bitcast.15), channel_id=1, replica_groups={{0,128,256,384},{1,129,257,385},{2,130,258,386},{3,131,259,387},{4,132,..., dimensions={0}, use_global_device_ids=true | all-gather | bytes 2560 | tf_op jit(solution)/shard_map/all_gather | solution.py:318
  74.1 0.0 all-to-all-done.3.parts_ref
  74.1 0.9 line_sums.1
  75.0 4.9 %all-to-all-start.4 = ((f32[4,128,256]{2,1,0:T(8,128)}), f32[4,128,256]{2,1,0:T(8,128)S(1)}, u32[]{:S(2)}, u32[]{:S(2)}) async-start(f32[4,128,256]{2,1,0:T(8,128)} %get-tuple-element.18), calls=%async_computation.4 | async-start | bytes 1048576 | tf_op jit(solution)/shard_map/all_to_all | solution.py:314
  79.9 9.5 %all-gather.1 = f32[4,1,128]{2,1,0:T(1,128)S(1)} all-gather(f32[1,1,128]{2,1,0:T(1,128)S(1)} %bitcast.16), channel_id=1, replica_groups={{0,32,64,96},{1,33,65,97},{2,34,66,98},{3,35,67,99},{4,36,68,100},{5,37..., dimensions={0}, use_global_device_ids=true | all-gather | bytes 2560 | tf_op jit(solution)/shard_map/all_gather | solution.py:318
  89.4 0.5 reduce_sum.19
  89.9 0.0 all-to-all-done.4
  89.9 0.7 mul.3
  (2 shorter events, 0.1 us)
Async XLA Ops:
  0.6 0.9 copy-start.1
  12.8 22.1 %copy-start.3 = (f32[2,2,32]{2,1,0:T(2,128)S(1)}, f32[2,2,32]{2,1,0:T(2,128)}, u32[]{:S(2)}) copy-start(f32[2,2,32]{2,1,0:T(2,128)} %rest_lse_ref.1) | copy-start | bytes 1540
  12.8 22.1 %copy-start.5 = (f32[2,2]{1,0:T(2,128)S(1)}, f32[2,2]{1,0:T(2,128)}, u32[]{:S(2)}) copy-start(f32[2,2]{1,0:T(2,128)} %ref_logp_ref.1) | copy-start | bytes 52
  12.8 22.1 %copy-start.7 = (f32[32]{0:T(128)S(1)}, f32[32]{0:T(128)}, u32[]{:S(2)}) copy-start(f32[32]{0:T(128)} %weight_of_ref.1) | copy-start | bytes 388
  13.0 21.9 %copy-start = (f32[4096,256]{1,0:T(8,128)S(1)}, f32[4096,256]{1,0:T(8,128)}, u32[]{:S(2)}) copy-start(f32[4096,256]{1,0:T(8,128)} %param.9) | copy-start | bytes 12582916
  13.0 21.9 %copy-start.2 = (s32[2,2,32]{2,1,0:T(2,128)S(1)}, s32[2,2,32]{2,1,0:T(2,128)}, u32[]{:S(2)}) copy-start(s32[2,2,32]{2,1,0:T(2,128)} %targets_ref.1) | copy-start | bytes 1540
  13.1 21.9 %copy-start.4 = (s32[2,2]{1,0:T(2,128)S(1)}, s32[2,2]{1,0:T(2,128)}, u32[]{:S(2)}) copy-start(s32[2,2]{1,0:T(2,128)} %lengths_ref.1) | copy-start | bytes 52
  13.1 21.9 %copy-start.6 = (s32[2]{0:T(128)S(1)}, s32[2]{0:T(128)}, u32[]{:S(2)}) copy-start(s32[2]{0:T(128)} %group_map_ref.1) | copy-start | bytes 28
  50.4 23.7 %all-to-all-start.3 = ((f32[4,4,128,256]{3,2,1,0:T(8,128)}), f32[4,4,128,256]{3,2,1,0:T(8,128)S(1)}, u32[]{:S(2)}, u32[]{:S(2)}) async-start(f32[4,4,128,256]{3,2,1,0:T(8,128)} %bitcast.17), calls=%async_computation.3 | async-start | bytes 4194304 | tf_op jit(solution)/shard_map/all_to_all | solution.py:314
  75.0 14.9 %all-to-all-start.4 = ((f32[4,128,256]{2,1,0:T(8,128)}), f32[4,128,256]{2,1,0:T(8,128)S(1)}, u32[]{:S(2)}, u32[]{:S(2)}) async-start(f32[4,128,256]{2,1,0:T(8,128)} %get-tuple-element.18), calls=%async_computation.4 | async-start | bytes 1048576 | tf_op jit(solution)/shard_map/all_to_all | solution.py:314

commit v4 on v3

--- a/solution.py
+++ b/solution.py
@@ -24,6 +24,14 @@
             places = [line * side + k if along_x else k * side + line for k in range(side)]
             groups.append([pair * holders + place for place in places])
     return groups
+
+
+def plane_groups(pairs, holders):
+    swapped = [(place % side) * side + place // side for place in range(holders)]
+    return [
+        [pair * holders + place for place in (range(holders) if pair % cores == 0 else swapped)]
+        for pair in range(pairs)
+    ]
 
 
 def chip_plane_groups(pairs, holders):
@@ -282,34 +290,6 @@
     )(stats, own, scaled, matches, weight_blocks)
 
 
-def line_sum_kernel(parts_ref, losses_ref, sums_ref, loss_ref, made_ref, sems):
-    loss_ref[...] = jnp.sum(losses_ref[...], axis=0, keepdims=True)
-    sent = []
-    for k in range(made_ref.shape[0]):
-        made_ref[k] = jnp.sum(parts_ref[:, k], axis=0)
-        sent.append(pltpu.make_async_copy(made_ref.at[k], sums_ref.at[k], sems.at[k]))
-        sent[k].start()
-    for copy in sent:
-        copy.wait()
-
-
-def line_sums(parts, loss_rows):
-    shape = parts.shape[1:]
-    in_vmem = pl.BlockSpec(memory_space=pltpu.VMEM)
-    return pl.pallas_call(
-        line_sum_kernel,
-        out_shape=(
-            pltpu.HBM(shape, jnp.float32),
-            jax.ShapeDtypeStruct((1, loss_rows.shape[1]), jnp.float32),
-        ),
-        in_specs=[in_vmem] * 2,
-        out_specs=(pl.BlockSpec(memory_space=pltpu.HBM), in_vmem),
-        scratch_shapes=[pltpu.VMEM(shape, jnp.float32), pltpu.SemaphoreType.DMA((shape[0],))],
-        compiler_params=pltpu.CompilerParams(vmem_limit_bytes=vmem_grant),
-        name="line_sums",
-    )(parts, loss_rows)
-
-
 def exchanged(blocks, groups):
     return lax.all_to_all(blocks, both_axes, 0, 0, axis_index_groups=groups, tiled=True)
 
@@ -337,12 +317,9 @@
     partial_rows, loss_row, token_grads = gradient_rows(
         pair_count, stats, own_stats, scaled, matches, weight_blocks
     )
-    line_parts = exchanged(
-        partial_rows.reshape(side, side, tokens, local_width), second_lines
-    )
+    summed_rows = jnp.sum(exchanged(partial_rows, plane_groups(pairs, holders)), axis=0)
     far_rows = gathered(loss_row, far_groups(pairs, holders))
-    line_rows, loss_row = line_sums(line_parts, far_rows)
-    summed_rows = jnp.sum(exchanged(line_rows, first_lines), axis=0)
+    loss_row = jnp.sum(far_rows, axis=0, keepdims=True)
     near_rows = gathered(loss_row, near_groups(pairs, holders))
     dpo_loss = jnp.sum(near_rows, axis=0)[0]
     return ((token_grads * summed_rows).reshape(hidden.shape), dpo_loss)

time: 91 us -> 86.7 us (0.953)
  the two profiles are of different devices: /device:TPU:10 before, /device:TPU:416 now
where the time goes in v4:
time: 86.7 us; the launch traced here: 86.5 us
  blocking collectives  66 us (76%)
  waiting for transfers between devices  9.06 us (10%)
  Pallas kernels  4.38 us (5%)
  starting transfers between devices  3.73 us (4%)
  other arithmetic  1.36 us (2%)
  local copies, waits for them, and re-layouts  1.13 us (1%)
    all_to_all x3, blocking collectives, exchanged(): lax.all_to_all(blocks, both_axes, 0, 0, axis_index_groups=groups, tiled=T...  44.3 us
    all_gather x2, blocking collectives, gathered(): lax.all_gather(row, both_axes, axis_index_groups=groups, axis=0, tiled=True)  21.8 us
    all_to_all x1, waiting for transfers between devices, exchanged(): lax.all_to_all(blocks, both_axes, 0, 0, axis_index_groups=groups, tiled=T...  9.06 us
    all_to_all x1, starting transfers between devices, exchanged(): lax.all_to_all(blocks, both_axes, 0, 0, axis_index_groups=groups, tiled=T...  3.73 us
    pallas_call x1, Pallas kernels, gradient_rows(): pl.pallas_call(functools.partial(rows_kernel, pair_count), out_shape=(plt...  2.4 us
    pallas_call x1, Pallas kernels, local_logits(): pl.pallas_call(logits_kernel, out_shape=(jax.ShapeDtypeStruct((columns, t...  1.95 us
  transfers between devices with their start and end apart: 1, of which 1 were waited for; matrix products, arithmetic and copies ran while one was open for 1% of the time, Pallas kernels for 0%

profile of v4, /device:TPU:416, one launch (start us, length us, event | category | flops | bytes accessed | tf_op | source)
XLA Modules:
  0.0 86.5 jit_solution(17623381260851961856)
XLA Ops:
  0.6 0.0 copy-start.1
  0.6 0.9 %copy-done.1 = f32[2,2,32,256]{3,2,1,0:T(8,128)S(1)} copy-done((f32[2,2,32,256]{3,2,1,0:T(8,128)S(1)}, f32[2,2,32,256]{3,2,1,0:T(8,128)}, u32[]{:S(2)}) %copy-start.1) | copy-done | bytes 131096
  1.6 12.2 %all_to_all.20 = f32[4,128,256]{2,1,0:T(8,128)S(1)} all-to-all(f32[4,128,256]{2,1,0:T(8,128)S(1)} %state_copies.1), channel_id=1, replica_groups={{0,1,2,3},{4,5,6,7},{8,9,10,11},{12,13,14,15},{16,20,24,28},{17,21,25,2..., dimensions={0} | all-to-all | bytes 1048576 | tf_op jit(solution)/shard_map/all_to_all | solution.py:294
  13.7 0.0 copy-start.3
  13.8 0.0 copy-start.5
  13.8 0.0 copy-start.7
  13.8 0.2 broadcast_in_dim.6
  14.0 0.0 copy-start
  14.0 0.0 copy-start.2
  14.0 0.0 copy-start.4
  14.0 0.0 copy-start.6
  14.0 21.0 %all_to_all.21 = f32[4,4,128,256]{3,2,1,0:T(8,128)S(1)} all-to-all(f32[4,4,128,256]{3,2,1,0:T(8,128)S(1)} %broadcast_in_dim.6), channel_id=1, replica_groups={{0,4,8,12},{1,5,9,13},{2,6,10,14},{3,7,11,15},{16,17,18,19},{20,21,22,2..., dimensions={0} | all-to-all | bytes 4194304 | tf_op jit(solution)/shard_map/all_to_all | solution.py:294
  35.0 0.0 copy-done.3
  35.1 0.0 copy-done.5
  35.1 0.0 copy-done.7
  35.1 0.0 copy-done
  35.1 0.0 copy-done.2
  35.1 0.0 copy-done.4
  35.1 0.0 copy-done.6
  35.1 1.9 %local_logits.1 = (f32[256,128]{1,0:T(8,128)S(1)}, f32[256,128]{1,0:T(8,128)S(1)}, f32[8,128]{1,0:T(8,128)S(1)}, f32[32,8,128]{2,1,0:T(8,128)S(1)}) custom-call(s32[2,2]{1,0:T(2,128)S(1)} %copy-done.4, f32[2,2]{1,0:T(2,128)S(1)} %copy-done.5, s32[2]{0:T(128)S(1)} %copy-done.6, f32[32]{0:T(128)S(1)} %copy-done.7, s32[2,2,32]{2,1,0:T(2,128)S(1)} %copy-done.2, ...), custom_call_target="tpu_custom_call" | custom-call | flops 805306368 | bytes 6291456 | tf_op jit(solution)/shard_map/local_logits/pallas_call | solution.py:174
  37.1 11.1 %all_to_all.22.stats_ref = f32[32,8,128]{2,1,0:T(8,128)S(1)} all-to-all(f32[32,8,128]{2,1,0:T(8,128)S(1)} %get-tuple-element.9), channel_id=1, replica_groups={{0,1,2,3,4,5,6,7,8,9,10,11,12,13,14,15,16,17,18,19,20,21,22,23,24,25,26..., dimensions={0} | all-to-all | bytes 262144 | tf_op jit(solution)/shard_map/all_to_all | solution.py:294
  48.1 2.4 %gradient_rows.1 = (f32[16,128,256]{2,1,0:T(8,128)}, f32[1,128]{1,0:T(1,128)S(1)}, f32[128,256]{1,0:T(8,128)S(1)}) custom-call(f32[32,8,128]{2,1,0:T(8,128)S(1)} %all_to_all.22.stats_ref, f32[8,128]{1,0:T(8,128)S(1)} %get-tuple-element.10.own_ref, f32[256,128]{1,0:T(8,128)S(1)} %get-tuple-element.11.scaled_ref, ...), custom_call_target="tpu_custom_call" | custom-call | flops 805306368 | bytes 6291456 | tf_op jit(solution)/shard_map/gradient_rows/pallas_call | solution.py:273
  50.5 3.7 %all-to-all-start.3 = ((f32[16,128,256]{2,1,0:T(8,128)}), f32[16,128,256]{2,1,0:T(8,128)S(1)}, u32[]{:S(2)}, u32[]{:S(2)}) async-start(f32[16,128,256]{2,1,0:T(8,128)} %get-tuple-element.14), calls=%async_computation.3 | async-start | bytes 4194304 | tf_op jit(solution)/shard_map/all_to_all | solution.py:294
  54.3 13.2 %all-gather.1 = f32[4,1,128]{2,1,0:T(1,128)S(1)} all-gather(f32[1,1,128]{2,1,0:T(1,128)S(1)} %bitcast.12), channel_id=1, replica_groups={{0,128,256,384},{1,129,257,385},{2,130,258,386},{3,131,259,387},{4,132,..., dimensions={0}, use_global_device_ids=true | all-gather | bytes 2560 | tf_op jit(solution)/shard_map/all_gather | solution.py:298
  67.5 8.6 %all-gather.2 = f32[4,1,128]{2,1,0:T(1,128)S(1)} all-gather(f32[1,1,128]{2,1,0:T(1,128)S(1)} %bitcast.14), channel_id=2, replica_groups={{0,32,64,96},{1,33,65,97},{2,34,66,98},{3,35,67,99},{4,36,68,100},{5,37..., dimensions={0}, use_global_device_ids=true | all-gather | bytes 2560 | tf_op jit(solution)/shard_map/all_gather | solution.py:298
  76.1 0.5 reduce_sum.29
  76.6 9.1 %all-to-all-done.3 = f32[16,128,256]{2,1,0:T(8,128)S(1)} async-done(((f32[16,128,256]{2,1,0:T(8,128)}), f32[16,128,256]{2,1,0:T(8,128)S(1)}, u32[]{:S(2)}, u32[]{:S(2)}) %all-to-all-start.3) | async-done | bytes 2097184 | tf_op jit(solution)/shard_map/all_to_all | solution.py:294
  85.7 0.1 reduce_sum.27
  85.8 0.7 mul.3
  (2 shorter events, 0.1 us)
Async XLA Ops:
  0.6 0.9 %copy-start.1 = (f32[2,2,32,256]{3,2,1,0:T(8,128)S(1)}, f32[2,2,32,256]{3,2,1,0:T(8,128)}, u32[]{:S(2)}) copy-start(f32[2,2,32,256]{3,2,1,0:T(8,128)} %param.8) | copy-start | bytes 393220
  13.7 21.3 %copy-start.3 = (f32[2,2,32]{2,1,0:T(2,128)S(1)}, f32[2,2,32]{2,1,0:T(2,128)}, u32[]{:S(2)}) copy-start(f32[2,2,32]{2,1,0:T(2,128)} %rest_lse_ref.1) | copy-start | bytes 1540
  13.8 21.3 %copy-start.5 = (f32[2,2]{1,0:T(2,128)S(1)}, f32[2,2]{1,0:T(2,128)}, u32[]{:S(2)}) copy-start(f32[2,2]{1,0:T(2,128)} %ref_logp_ref.1) | copy-start | bytes 52
  13.8 21.3 %copy-start.7 = (f32[32]{0:T(128)S(1)}, f32[32]{0:T(128)}, u32[]{:S(2)}) copy-start(f32[32]{0:T(128)} %weight_of_ref.1) | copy-start | bytes 388
  14.0 21.1 %copy-start = (f32[4096,256]{1,0:T(8,128)S(1)}, f32[4096,256]{1,0:T(8,128)}, u32[]{:S(2)}) copy-start(f32[4096,256]{1,0:T(8,128)} %param.9) | copy-start | bytes 12582916
  14.0 21.1 %copy-start.2 = (s32[2,2,32]{2,1,0:T(2,128)S(1)}, s32[2,2,32]{2,1,0:T(2,128)}, u32[]{:S(2)}) copy-start(s32[2,2,32]{2,1,0:T(2,128)} %targets_ref.1) | copy-start | bytes 1540
  14.0 21.1 %copy-start.4 = (s32[2,2]{1,0:T(2,128)S(1)}, s32[2,2]{1,0:T(2,128)}, u32[]{:S(2)}) copy-start(s32[2,2]{1,0:T(2,128)} %lengths_ref.1) | copy-start | bytes 52
  14.0 21.1 %copy-start.6 = (s32[2]{0:T(128)S(1)}, s32[2]{0:T(128)}, u32[]{:S(2)}) copy-start(s32[2]{0:T(128)} %group_map_ref.1) | copy-start | bytes 28
  50.5 35.1 %all-to-all-start.3 = ((f32[16,128,256]{2,1,0:T(8,128)}), f32[16,128,256]{2,1,0:T(8,128)S(1)}, u32[]{:S(2)}, u32[]{:S(2)}) async-start(f32[16,128,256]{2,1,0:T(8,128)} %get-tuple-element.14), calls=%async_computation.3 | async-start | bytes 4194304 | tf_op jit(solution)/shard_map/all_to_all | solution.py:294

commit v5 on v4

--- a/solution.py
+++ b/solution.py
@@ -129,21 +129,21 @@
     target_row = token_row(targets_ref)
     token = lax.broadcasted_iota(jnp.int32, target_row.shape, 1)
     slot, sequence = token % seq_slots, token // seq_slots
-    divisor = 0.0
-    for k in range(weight_of_ref.shape[0]):
-        divisor += weight_of_ref[k]
-    divisor = pair_count * divisor
-    live = jnp.zeros(target_row.shape, jnp.float32)
+    group_weights = weight_of_ref[...]
+    group_ids = lax.broadcasted_iota(jnp.int32, group_weights.shape, 1)
+    divisor = pair_count * jnp.sum(group_weights, axis=1, keepdims=True)
+    count = jnp.zeros(target_row.shape, jnp.int32)
     prior = jnp.zeros(target_row.shape, jnp.float32)
     share = jnp.zeros(target_row.shape, jnp.float32)
     for pair in range(pair_count):
-        pair_share = weight_of_ref[group_map_ref[pair]]
+        chosen_group = group_ids == group_map_ref[0:1, pair : pair + 1]
+        pair_weight = jnp.sum(jnp.where(chosen_group, group_weights, 0.0), axis=1, keepdims=True)
+        share = jnp.where(sequence // 2 == pair, pair_weight / divisor, share)
         for one in range(2):
             here = sequence == 2 * pair + one
-            live = jnp.where(here & (slot < lengths_ref[pair, one]), 1.0, live)
-            prior = jnp.where(here, ref_logp_ref[pair, one], prior)
-            share = jnp.where(here, pair_share, share)
-    share = share / divisor
+            count = jnp.where(here, lengths_ref[pair : pair + 1, one : one + 1], count)
+            prior = jnp.where(here, ref_logp_ref[pair : pair + 1, one : one + 1], prior)
+    live = jnp.where(slot < count, 1.0, 0.0)
 
     own_core = lax.axis_index("dp") % cores
     total = product(stacked_parts(states_ref[0]), weight_ref[0], 0)
@@ -167,7 +167,7 @@
         stats_ref[k] = stats
 
 
-def local_logits(scalars, targets, rest_lse, states, weight_blocks):
+def local_logits(small, targets, rest_lse, states, weight_blocks):
     holders, tokens, _ = states.shape
     columns = weight_blocks.shape[2]
     in_vmem = pl.BlockSpec(memory_space=pltpu.VMEM)
@@ -179,7 +179,7 @@
             jax.ShapeDtypeStruct((stat_rows, tokens), jnp.float32),
             jax.ShapeDtypeStruct((cores * holders, stat_rows, tokens), jnp.float32),
         ),
-        in_specs=[pl.BlockSpec(memory_space=pltpu.SMEM)] * len(scalars) + [in_vmem] * 4,
+        in_specs=[in_vmem] * (len(small) + 4),
         out_specs=(in_vmem,) * 4,
         compiler_params=pltpu.CompilerParams(vmem_limit_bytes=vmem_grant),
         cost_estimate=pl.CostEstimate(
@@ -188,7 +188,7 @@
             transcendentals=tokens * columns,
         ),
         name="local_logits",
-    )(*scalars, targets, rest_lse, states, weight_blocks)
+    )(*small, targets, rest_lse, states, weight_blocks)
 
 
 def softplus(values):
@@ -246,11 +246,6 @@
     full_lse, _ = joined(stats_ref[mine])
     scale = jnp.exp(own_ref[0:1] - full_lse)
     both = stacked_parts((matches_ref[...] - scale * scaled_ref[...]).T)
-    sent = []
-    for k in range(holders):
-        made_ref[k] = product(both, weight_ref[holder_of(k, own_core)], 1)
-        sent.append(pltpu.make_async_copy(made_ref.at[k], rows_ref.at[k], sems.at[k]))
-        sent[k].start()
     loss = jnp.zeros((1, 1), jnp.float32)
     token_grad = jnp.zeros(loss_ref.shape, jnp.float32)
     for core in range(cores):
@@ -261,6 +256,11 @@
         token_grad = jnp.where(own_core == core, core_grad, token_grad)
     loss_ref[...] = jnp.broadcast_to(loss, loss_ref.shape)
     grads_ref[...] = jnp.broadcast_to(token_grad, grads_ref.shape[::-1]).T
+    sent = []
+    for k in range(holders):
+        made_ref[k] = product(both, weight_ref[holder_of(k, own_core)], 1)
+        sent.append(pltpu.make_async_copy(made_ref.at[k], rows_ref.at[k], sems.at[k]))
+        sent[k].start()
     for copy in sent:
         copy.wait()
 
@@ -311,7 +311,7 @@
     states = exchanged(jnp.broadcast_to(near, (side, *near.shape)), second_lines)
     states = states.reshape(holders, tokens, local_width)
     scaled, matches, own_stats, stat_copies = local_logits(
-        (lengths, ref_logp, group_map, group_weight), targets, rest_lse, states, weight_blocks
+        (lengths, ref_logp, group_map.reshape(1, -1), group_weight.reshape(1, -1)), targets, rest_lse, states, weight_blocks
     )
     stats = exchanged(stat_copies, chip_plane_groups(pairs, holders))
     partial_rows, loss_row, token_grads = gradient_rows(

time: 86.7 us -> 86.1 us (level)
  the two profiles are of different devices: /device:TPU:416 before, /device:TPU:224 now
where the time goes in v5:
time: 86.1 us; the launch traced here: 85.8 us
  blocking collectives  66.1 us (77%)
  waiting for transfers between devices  9.02 us (10%)
  starting transfers between devices  3.73 us (4%)
  Pallas kernels  3.72 us (4%)
  other arithmetic  1.36 us (2%)
  local copies, waits for them, and re-layouts  1.14 us (1%)
    all_to_all x3, blocking collectives, exchanged(): lax.all_to_all(blocks, both_axes, 0, 0, axis_index_groups=groups, tiled=T...  44.3 us
    all_gather x2, blocking collectives, gathered(): lax.all_gather(row, both_axes, axis_index_groups=groups, axis=0, tiled=True)  21.8 us
    all_to_all x1, waiting for transfers between devices, exchanged(): lax.all_to_all(blocks, both_axes, 0, 0, axis_index_groups=groups, tiled=T...  9.02 us
    all_to_all x1, starting transfers between devices, exchanged(): lax.all_to_all(blocks, both_axes, 0, 0, axis_index_groups=groups, tiled=T...  3.73 us
    pallas_call x1, Pallas kernels, gradient_rows(): pl.pallas_call(functools.partial(rows_kernel, pair_count), out_shape=(plt...  2.4 us
  transfers between devices with their start and end apart: 1, of which 1 were waited for; matrix products, arithmetic and copies ran while one was open for 1% of the time, Pallas kernels for 0%

profile of v5, /device:TPU:224, one launch (start us, length us, event | category | flops | bytes accessed | tf_op | source)
XLA Modules:
  0.0 85.8 jit_solution(52588512071053964)
XLA Ops:
  0.6 0.0 copy-start.1
  0.6 0.9 %copy-done.1 = f32[2,2,32,256]{3,2,1,0:T(8,128)S(1)} copy-done((f32[2,2,32,256]{3,2,1,0:T(8,128)S(1)}, f32[2,2,32,256]{3,2,1,0:T(8,128)}, u32[]{:S(2)}) %copy-start.1) | copy-done | bytes 131096
  1.6 12.2 %all_to_all.20 = f32[4,128,256]{2,1,0:T(8,128)S(1)} all-to-all(f32[4,128,256]{2,1,0:T(8,128)S(1)} %state_copies.1), channel_id=1, replica_groups={{0,1,2,3},{4,5,6,7},{8,9,10,11},{12,13,14,15},{16,20,24,28},{17,21,25,2..., dimensions={0} | all-to-all | bytes 1048576 | tf_op jit(solution)/shard_map/all_to_all | solution.py:294
  13.7 0.2 broadcast_in_dim.6
  14.0 0.0 copy-start
  14.0 0.0 copy-start.2
  14.0 0.0 copy-start.3
  14.0 0.0 copy-start.4
  14.0 0.0 copy-start.5
  14.0 0.0 copy-start.6
  14.0 0.0 copy-start.7
  14.0 21.0 %all_to_all.21 = f32[4,4,128,256]{3,2,1,0:T(8,128)S(1)} all-to-all(f32[4,4,128,256]{3,2,1,0:T(8,128)S(1)} %broadcast_in_dim.6), channel_id=1, replica_groups={{0,4,8,12},{1,5,9,13},{2,6,10,14},{3,7,11,15},{16,17,18,19},{20,21,22,2..., dimensions={0} | all-to-all | bytes 4194304 | tf_op jit(solution)/shard_map/all_to_all | solution.py:294
  35.1 0.0 copy-done
  35.1 0.0 copy-done.2
  35.1 0.0 copy-done.3
  35.1 0.0 copy-done.4
  35.1 0.0 copy-done.5
  35.1 0.0 copy-done.6
  35.1 0.0 copy-done.7
  35.1 1.3 %local_logits.1 = (f32[256,128]{1,0:T(8,128)S(1)}, f32[256,128]{1,0:T(8,128)S(1)}, f32[8,128]{1,0:T(8,128)S(1)}, f32[32,8,128]{2,1,0:T(8,128)S(1)}) custom-call(s32[2,2]{1,0:T(2,128)S(1)} %copy-done.4, f32[2,2]{1,0:T(2,128)S(1)} %copy-done.5, s32[1,2]{1,0:T(1,128)S(1)} %bitcast.14, f32[1,32]{1,0:T(1,128)S(1)} %bitcast.15, s32[2,2,32]{2,1,0:T(2,128)S(1)} %copy-done.2, ...), custom_call_target="tpu_custom_call" | custom-call | flops 805306368 | bytes 6291456 | tf_op jit(solution)/shard_map/local_logits/pallas_call | solution.py:174
  36.4 11.1 %all_to_all.22.stats_ref = f32[32,8,128]{2,1,0:T(8,128)S(1)} all-to-all(f32[32,8,128]{2,1,0:T(8,128)S(1)} %get-tuple-element.9), channel_id=1, replica_groups={{0,1,2,3,4,5,6,7,8,9,10,11,12,13,14,15,16,17,18,19,20,21,22,23,24,25,26..., dimensions={0} | all-to-all | bytes 262144 | tf_op jit(solution)/shard_map/all_to_all | solution.py:294
  47.5 2.4 %gradient_rows.1 = (f32[16,128,256]{2,1,0:T(8,128)}, f32[1,128]{1,0:T(1,128)S(1)}, f32[128,256]{1,0:T(8,128)S(1)}) custom-call(f32[32,8,128]{2,1,0:T(8,128)S(1)} %all_to_all.22.stats_ref, f32[8,128]{1,0:T(8,128)S(1)} %get-tuple-element.10.own_ref, f32[256,128]{1,0:T(8,128)S(1)} %get-tuple-element.11.scaled_ref, ...), custom_call_target="tpu_custom_call" | custom-call | flops 805306368 | bytes 6291456 | tf_op jit(solution)/shard_map/gradient_rows/pallas_call | solution.py:273
  49.9 3.7 %all-to-all-start.3 = ((f32[16,128,256]{2,1,0:T(8,128)}), f32[16,128,256]{2,1,0:T(8,128)S(1)}, u32[]{:S(2)}, u32[]{:S(2)}) async-start(f32[16,128,256]{2,1,0:T(8,128)} %get-tuple-element.14), calls=%async_computation.3 | async-start | bytes 4194304 | tf_op jit(solution)/shard_map/all_to_all | solution.py:294
  53.6 14.2 %all-gather.1 = f32[4,1,128]{2,1,0:T(1,128)S(1)} all-gather(f32[1,1,128]{2,1,0:T(1,128)S(1)} %bitcast.16), channel_id=1, replica_groups={{0,128,256,384},{1,129,257,385},{2,130,258,386},{3,131,259,387},{4,132,..., dimensions={0}, use_global_device_ids=true | all-gather | bytes 2560 | tf_op jit(solution)/shard_map/all_gather | solution.py:298
  67.8 7.6 %all-gather.2 = f32[4,1,128]{2,1,0:T(1,128)S(1)} all-gather(f32[1,1,128]{2,1,0:T(1,128)S(1)} %bitcast.18), channel_id=2, replica_groups={{0,32,64,96},{1,33,65,97},{2,34,66,98},{3,35,67,99},{4,36,68,100},{5,37..., dimensions={0}, use_global_device_ids=true | all-gather | bytes 2560 | tf_op jit(solution)/shard_map/all_gather | solution.py:298
  75.5 0.5 reduce_sum.29
  76.0 9.0 %all-to-all-done.3 = f32[16,128,256]{2,1,0:T(8,128)S(1)} async-done(((f32[16,128,256]{2,1,0:T(8,128)}), f32[16,128,256]{2,1,0:T(8,128)S(1)}, u32[]{:S(2)}, u32[]{:S(2)}) %all-to-all-start.3) | async-done | bytes 2097184 | tf_op jit(solution)/shard_map/all_to_all | solution.py:294
  85.0 0.1 reduce_sum.27
  85.1 0.7 mul.3
  (2 shorter events, 0.1 us)
Async XLA Ops:
  0.6 0.9 %copy-start.1 = (f32[2,2,32,256]{3,2,1,0:T(8,128)S(1)}, f32[2,2,32,256]{3,2,1,0:T(8,128)}, u32[]{:S(2)}) copy-start(f32[2,2,32,256]{3,2,1,0:T(8,128)} %param.8) | copy-start | bytes 393220
  14.0 21.1 %copy-start = (f32[4096,256]{1,0:T(8,128)S(1)}, f32[4096,256]{1,0:T(8,128)}, u32[]{:S(2)}) copy-start(f32[4096,256]{1,0:T(8,128)} %param.9) | copy-start | bytes 12582916
  14.0 21.1 %copy-start.2 = (s32[2,2,32]{2,1,0:T(2,128)S(1)}, s32[2,2,32]{2,1,0:T(2,128)}, u32[]{:S(2)}) copy-start(s32[2,2,32]{2,1,0:T(2,128)} %targets_ref.1) | copy-start | bytes 1540
  14.0 21.1 %copy-start.3 = (f32[2,2,32]{2,1,0:T(2,128)S(1)}, f32[2,2,32]{2,1,0:T(2,128)}, u32[]{:S(2)}) copy-start(f32[2,2,32]{2,1,0:T(2,128)} %rest_lse_ref.1) | copy-start | bytes 1540
  14.0 21.1 %copy-start.4 = (s32[2,2]{1,0:T(2,128)S(1)}, s32[2,2]{1,0:T(2,128)}, u32[]{:S(2)}) copy-start(s32[2,2]{1,0:T(2,128)} %lengths_ref.1) | copy-start | bytes 52
  14.0 21.1 %copy-start.5 = (f32[2,2]{1,0:T(2,128)S(1)}, f32[2,2]{1,0:T(2,128)}, u32[]{:S(2)}) copy-start(f32[2,2]{1,0:T(2,128)} %ref_logp_ref.1) | copy-start | bytes 52
  14.0 21.1 %copy-start.6 = (s32[2]{0:T(128)S(1)}, s32[2]{0:T(128)}, u32[]{:S(2)}) copy-start(s32[2]{0:T(128)} %param.14) | copy-start | bytes 28
  14.0 21.1 %copy-start.7 = (f32[32]{0:T(128)S(1)}, f32[32]{0:T(128)}, u32[]{:S(2)}) copy-start(f32[32]{0:T(128)} %param.15) | copy-start | bytes 388
  49.9 35.1 %all-to-all-start.3 = ((f32[16,128,256]{2,1,0:T(8,128)}), f32[16,128,256]{2,1,0:T(8,128)S(1)}, u32[]{:S(2)}, u32[]{:S(2)}) async-start(f32[16,128,256]{2,1,0:T(8,128)} %get-tuple-element.14), calls=%async_computation.3 | async-start | bytes 4194304 | tf_op jit(solution)/shard_map/all_to_all | solution.py:294

commit v6 on v5

--- a/solution.py
+++ b/solution.py
@@ -13,6 +13,7 @@
 side = 4
 near_chips = 4
 stat_rows = 8
+closing_steps = 4
 vmem_grant = 24 * 1024 * 1024
 
 
@@ -26,12 +27,16 @@
     return groups
 
 
+def snake(holders):
+    return [
+        line * side + (k if line % 2 == 0 else side - 1 - k)
+        for line in range(holders // side)
+        for k in range(side)
+    ]
+
+
 def plane_groups(pairs, holders):
-    swapped = [(place % side) * side + place // side for place in range(holders)]
-    return [
-        [pair * holders + place for place in (range(holders) if pair % cores == 0 else swapped)]
-        for pair in range(pairs)
-    ]
+    return [[pair * holders + place for place in snake(holders)] for pair in range(pairs)]
 
 
 def chip_plane_groups(pairs, holders):
@@ -257,8 +262,8 @@
     loss_ref[...] = jnp.broadcast_to(loss, loss_ref.shape)
     grads_ref[...] = jnp.broadcast_to(token_grad, grads_ref.shape[::-1]).T
     sent = []
-    for k in range(holders):
-        made_ref[k] = product(both, weight_ref[holder_of(k, own_core)], 1)
+    for k, place in enumerate(snake(holders)):
+        made_ref[k] = product(both, weight_ref[place], 1)
         sent.append(pltpu.make_async_copy(made_ref.at[k], rows_ref.at[k], sems.at[k]))
         sent[k].start()
     for copy in sent:
@@ -290,6 +295,39 @@
     )(stats, own, scaled, matches, weight_blocks)
 
 
+def closing_kernel(parts_ref, factors_ref, losses_ref, grad_ref, loss_ref, made_ref, total_ref, sems):
+    total_ref[...] = jnp.sum(losses_ref[...], axis=0, keepdims=True)
+    sent = [pltpu.make_async_copy(total_ref, loss_ref, sems.at[closing_steps])]
+    sent[0].start()
+    rows = made_ref.shape[0] // closing_steps
+    for k in range(closing_steps):
+        part = pl.ds(k * rows, rows)
+        made_ref[part] = factors_ref[part] * jnp.sum(parts_ref[:, part], axis=0)
+        sent.append(pltpu.make_async_copy(made_ref.at[part], grad_ref.at[part], sems.at[k]))
+        sent[-1].start()
+    for copy in sent:
+        copy.wait()
+
+
+def closed(parts, factors, losses):
+    shape, loss_shape = factors.shape, (1, losses.shape[1])
+    in_vmem = pl.BlockSpec(memory_space=pltpu.VMEM)
+    in_hbm = pl.BlockSpec(memory_space=pltpu.HBM)
+    return pl.pallas_call(
+        closing_kernel,
+        out_shape=(pltpu.HBM(shape, jnp.float32), pltpu.HBM(loss_shape, jnp.float32)),
+        in_specs=[in_vmem] * 3,
+        out_specs=(in_hbm, in_hbm),
+        scratch_shapes=[
+            pltpu.VMEM(shape, jnp.float32),
+            pltpu.VMEM(loss_shape, jnp.float32),
+            pltpu.SemaphoreType.DMA((closing_steps + 1,)),
+        ],
+        compiler_params=pltpu.CompilerParams(vmem_limit_bytes=vmem_grant),
+        name="closing",
+    )(parts, factors, losses)
+
+
 def exchanged(blocks, groups):
     return lax.all_to_all(blocks, both_axes, 0, 0, axis_index_groups=groups, tiled=True)
 
@@ -317,12 +355,12 @@
     partial_rows, loss_row, token_grads = gradient_rows(
         pair_count, stats, own_stats, scaled, matches, weight_blocks
     )
-    summed_rows = jnp.sum(exchanged(partial_rows, plane_groups(pairs, holders)), axis=0)
+    row_parts = exchanged(partial_rows, plane_groups(pairs, holders))
     far_rows = gathered(loss_row, far_groups(pairs, holders))
     loss_row = jnp.sum(far_rows, axis=0, keepdims=True)
     near_rows = gathered(loss_row, near_groups(pairs, holders))
-    dpo_loss = jnp.sum(near_rows, axis=0)[0]
-    return ((token_grads * summed_rows).reshape(hidden.shape), dpo_loss)
+    hidden_grad, total_row = closed(row_parts, token_grads, near_rows)
+    return (hidden_grad.reshape(hidden.shape), total_row[0, 0])
 
 
 def solution(mesh):

time: 86.1 us -> 86.4 us (level)
  the two profiles are of different devices: /device:TPU:224 before, /device:TPU:1 now
where the time goes in v6:
time: 86.4 us; the launch traced here: 86.1 us
  blocking collectives  71.8 us (83%)
  Pallas kernels  4.53 us (5%)
  waiting for transfers between devices  4.18 us (5%)
  starting transfers between devices  3.73 us (4%)
  local copies, waits for them, and re-layouts  1.14 us (1%)
    all_to_all x3, blocking collectives, exchanged(): lax.all_to_all(blocks, both_axes, 0, 0, axis_index_groups=groups, tiled=T...  47.1 us
    all_gather x2, blocking collectives, gathered(): lax.all_gather(row, both_axes, axis_index_groups=groups, axis=0, tiled=True)  24.7 us
    all_to_all x1, waiting for transfers between devices, exchanged(): lax.all_to_all(blocks, both_axes, 0, 0, axis_index_groups=groups, tiled=T...  4.18 us
    all_to_all x1, starting transfers between devices, exchanged(): lax.all_to_all(blocks, both_axes, 0, 0, axis_index_groups=groups, tiled=T...  3.73 us
    pallas_call x1, Pallas kernels, gradient_rows(): pl.pallas_call(functools.partial(rows_kernel, pair_count), out_shape=(plt...  2.44 us
  transfers between devices with their start and end apart: 1, of which 1 were waited for; matrix products, arithmetic and copies ran while one was open for 0% of the time, Pallas kernels for 0%

profile of v6, /device:TPU:1, one launch (start us, length us, event | category | flops | bytes accessed | tf_op | source)
XLA Modules:
  0.0 86.1 jit_solution(4289118094146124785)
XLA Ops:
  0.6 0.0 copy-start.1
  0.6 0.9 %copy-done.1 = f32[2,2,32,256]{3,2,1,0:T(8,128)S(1)} copy-done((f32[2,2,32,256]{3,2,1,0:T(8,128)S(1)}, f32[2,2,32,256]{3,2,1,0:T(8,128)}, u32[]{:S(2)}) %copy-start.1) | copy-done | bytes 131096
  1.6 11.7 %all_to_all.20 = f32[4,128,256]{2,1,0:T(8,128)S(1)} all-to-all(f32[4,128,256]{2,1,0:T(8,128)S(1)} %state_copies.1), channel_id=1, replica_groups={{0,1,2,3},{4,5,6,7},{8,9,10,11},{12,13,14,15},{16,20,24,28},{17,21,25,2..., dimensions={0} | all-to-all | bytes 1048576 | tf_op jit(solution)/shard_map/all_to_all | solution.py:332
  13.3 0.2 broadcast_in_dim.6
  13.5 0.0 copy-start
  13.5 0.0 copy-start.2
  13.5 0.0 copy-start.3
  13.6 0.0 copy-start.4
  13.6 0.0 copy-start.5
  13.6 0.0 copy-start.6
  13.6 0.0 copy-start.7
  13.6 19.5 %all_to_all.21 = f32[4,4,128,256]{3,2,1,0:T(8,128)S(1)} all-to-all(f32[4,4,128,256]{3,2,1,0:T(8,128)S(1)} %broadcast_in_dim.6), channel_id=1, replica_groups={{0,4,8,12},{1,5,9,13},{2,6,10,14},{3,7,11,15},{16,17,18,19},{20,21,22,2..., dimensions={0} | all-to-all | bytes 4194304 | tf_op jit(solution)/shard_map/all_to_all | solution.py:332
  33.1 0.0 copy-done
  33.1 0.0 copy-done.2
  33.1 0.0 copy-done.3
  33.1 0.0 copy-done.4
  33.1 0.0 copy-done.5
  33.1 0.0 copy-done.6
  33.2 0.0 copy-done.7
  33.2 1.3 %local_logits.1 = (f32[256,128]{1,0:T(8,128)S(1)}, f32[256,128]{1,0:T(8,128)S(1)}, f32[8,128]{1,0:T(8,128)S(1)}, f32[32,8,128]{2,1,0:T(8,128)S(1)}) custom-call(s32[2,2]{1,0:T(2,128)S(1)} %copy-done.4, f32[2,2]{1,0:T(2,128)S(1)} %copy-done.5, s32[1,2]{1,0:T(1,128)S(1)} %bitcast.16, f32[1,32]{1,0:T(1,128)S(1)} %bitcast.17, s32[2,2,32]{2,1,0:T(2,128)S(1)} %copy-done.2, ...), custom_call_target="tpu_custom_call" | custom-call | flops 805306368 | bytes 6291456 | tf_op jit(solution)/shard_map/local_logits/pallas_call | solution.py:179
  34.5 15.8 %all_to_all.22.stats_ref = f32[32,8,128]{2,1,0:T(8,128)S(1)} all-to-all(f32[32,8,128]{2,1,0:T(8,128)S(1)} %get-tuple-element.11), channel_id=1, replica_groups={{0,1,2,3,4,5,6,7,8,9,10,11,12,13,14,15,16,17,18,19,20,21,22,23,24,25,26..., dimensions={0} | all-to-all | bytes 262144 | tf_op jit(solution)/shard_map/all_to_all | solution.py:332
  50.3 2.4 %gradient_rows.1 = (f32[16,128,256]{2,1,0:T(8,128)}, f32[1,128]{1,0:T(1,128)S(1)}, f32[128,256]{1,0:T(8,128)S(1)}) custom-call(f32[32,8,128]{2,1,0:T(8,128)S(1)} %all_to_all.22.stats_ref, f32[8,128]{1,0:T(8,128)S(1)} %get-tuple-element.12.own_ref, f32[256,128]{1,0:T(8,128)S(1)} %get-tuple-element.13.scaled_ref, ...), custom_call_target="tpu_custom_call" | custom-call | flops 805306368 | bytes 6291456 | tf_op jit(solution)/shard_map/gradient_rows/pallas_call | solution.py:278
  52.7 3.7 %all-to-all-start.3 = ((f32[16,128,256]{2,1,0:T(8,128)}), f32[16,128,256]{2,1,0:T(8,128)S(1)}, u32[]{:S(2)}, u32[]{:S(2)}) async-start(f32[16,128,256]{2,1,0:T(8,128)} %get-tuple-element.15), calls=%async_computation.3 | async-start | bytes 4194304 | tf_op jit(solution)/shard_map/all_to_all | solution.py:332
  56.5 16.9 %all-gather.1 = f32[4,1,128]{2,1,0:T(1,128)S(1)} all-gather(f32[1,1,128]{2,1,0:T(1,128)S(1)} %bitcast.18), channel_id=1, replica_groups={{0,128,256,384},{1,129,257,385},{2,130,258,386},{3,131,259,387},{4,132,..., dimensions={0}, use_global_device_ids=true | all-gather | bytes 2560 | tf_op jit(solution)/shard_map/all_gather | solution.py:336
  73.4 7.8 %all-gather.2 = f32[4,1,128]{2,1,0:T(1,128)S(1)} all-gather(f32[1,1,128]{2,1,0:T(1,128)S(1)} %bitcast.19), channel_id=2, replica_groups={{0,32,64,96},{1,33,65,97},{2,34,66,98},{3,35,67,99},{4,36,68,100},{5,37..., dimensions={0}, use_global_device_ids=true | all-gather | bytes 2560 | tf_op jit(solution)/shard_map/all_gather | solution.py:336
  81.2 4.2 %all-to-all-done.3.parts_ref = f32[16,128,256]{2,1,0:T(8,128)S(1)} async-done(((f32[16,128,256]{2,1,0:T(8,128)}), f32[16,128,256]{2,1,0:T(8,128)S(1)}, u32[]{:S(2)}, u32[]{:S(2)}) %all-to-all-start.3) | async-done | bytes 2097184 | tf_op jit(solution)/shard_map/all_to_all | solution.py:332
  85.4 0.8 closing.1
  (2 shorter events, 0.1 us)
Async XLA Ops:
  0.6 0.9 %copy-start.1 = (f32[2,2,32,256]{3,2,1,0:T(8,128)S(1)}, f32[2,2,32,256]{3,2,1,0:T(8,128)}, u32[]{:S(2)}) copy-start(f32[2,2,32,256]{3,2,1,0:T(8,128)} %param.8) | copy-start | bytes 393220
  13.5 19.6 %copy-start = (f32[4096,256]{1,0:T(8,128)S(1)}, f32[4096,256]{1,0:T(8,128)}, u32[]{:S(2)}) copy-start(f32[4096,256]{1,0:T(8,128)} %param.9) | copy-start | bytes 12582916
  13.5 19.6 %copy-start.2 = (s32[2,2,32]{2,1,0:T(2,128)S(1)}, s32[2,2,32]{2,1,0:T(2,128)}, u32[]{:S(2)}) copy-start(s32[2,2,32]{2,1,0:T(2,128)} %targets_ref.1) | copy-start | bytes 1540
  13.5 19.6 %copy-start.3 = (f32[2,2,32]{2,1,0:T(2,128)S(1)}, f32[2,2,32]{2,1,0:T(2,128)}, u32[]{:S(2)}) copy-start(f32[2,2,32]{2,1,0:T(2,128)} %rest_lse_ref.1) | copy-start | bytes 1540
  13.6 19.6 %copy-start.4 = (s32[2,2]{1,0:T(2,128)S(1)}, s32[2,2]{1,0:T(2,128)}, u32[]{:S(2)}) copy-start(s32[2,2]{1,0:T(2,128)} %lengths_ref.1) | copy-start | bytes 52
  13.6 19.6 %copy-start.5 = (f32[2,2]{1,0:T(2,128)S(1)}, f32[2,2]{1,0:T(2,128)}, u32[]{:S(2)}) copy-start(f32[2,2]{1,0:T(2,128)} %ref_logp_ref.1) | copy-start | bytes 52
  13.6 19.6 %copy-start.6 = (s32[2]{0:T(128)S(1)}, s32[2]{0:T(128)}, u32[]{:S(2)}) copy-start(s32[2]{0:T(128)} %param.14) | copy-start | bytes 28
  13.6 19.6 %copy-start.7 = (f32[32]{0:T(128)S(1)}, f32[32]{0:T(128)}, u32[]{:S(2)}) copy-start(f32[32]{0:T(128)} %param.15) | copy-start | bytes 388
  52.7 32.6 %all-to-all-start.3 = ((f32[16,128,256]{2,1,0:T(8,128)}), f32[16,128,256]{2,1,0:T(8,128)S(1)}, u32[]{:S(2)}, u32[]{:S(2)}) async-start(f32[16,128,256]{2,1,0:T(8,128)} %get-tuple-element.15), calls=%async_computation.3 | async-start | bytes 4194304 | tf_op jit(solution)/shard_map/all_to_all | solution.py:332

commit v7 on v6

--- a/solution.py
+++ b/solution.py
@@ -35,8 +35,15 @@
     ]
 
 
+def by_columns(holders):
+    return [(place % side) * side + place // side for place in range(holders)]
+
+
 def plane_groups(pairs, holders):
-    return [[pair * holders + place for place in snake(holders)] for pair in range(pairs)]
+    orders = (snake(holders), by_columns(holders))
+    return [
+        [pair * holders + place for place in orders[pair % cores]] for pair in range(pairs)
+    ]
 
 
 def chip_plane_groups(pairs, holders):
@@ -262,8 +269,8 @@
     loss_ref[...] = jnp.broadcast_to(loss, loss_ref.shape)
     grads_ref[...] = jnp.broadcast_to(token_grad, grads_ref.shape[::-1]).T
     sent = []
-    for k, place in enumerate(snake(holders)):
-        made_ref[k] = product(both, weight_ref[place], 1)
+    for k, (even, odd) in enumerate(zip(snake(holders), by_columns(holders))):
+        made_ref[k] = product(both, weight_ref[jnp.where(own_core == 0, even, odd)], 1)
         sent.append(pltpu.make_async_copy(made_ref.at[k], rows_ref.at[k], sems.at[k]))
         sent[k].start()
     for copy in sent:

time: 86.4 us -> 86 us (level)
  no operation moved by 1% of the time
where the time goes in v7:
time: 86 us; the launch traced here: 85.7 us
  blocking collectives  72.1 us (84%)
  Pallas kernels  4.51 us (5%)
  starting transfers between devices  3.73 us (4%)
  waiting for transfers between devices  3.46 us (4%)
  local copies, waits for them, and re-layouts  1.14 us (1%)
    all_to_all x3, blocking collectives, exchanged(): lax.all_to_all(blocks, both_axes, 0, 0, axis_index_groups=groups, tiled=T...  47.1 us
    all_gather x2, blocking collectives, gathered(): lax.all_gather(row, both_axes, axis_index_groups=groups, axis=0, tiled=True)  25 us
    all_to_all x1, starting transfers between devices, exchanged(): lax.all_to_all(blocks, both_axes, 0, 0, axis_index_groups=groups, tiled=T...  3.73 us
    all_to_all x1, waiting for transfers between devices, exchanged(): lax.all_to_all(blocks, both_axes, 0, 0, axis_index_groups=groups, tiled=T...  3.46 us
    pallas_call x1, Pallas kernels, gradient_rows(): pl.pallas_call(functools.partial(rows_kernel, pair_count), out_shape=(plt...  2.43 us
  transfers between devices with their start and end apart: 1, of which 1 were waited for; matrix products, arithmetic and copies ran while one was open for 0% of the time, Pallas kernels for 0%

profile of v7, /device:TPU:1, one launch (start us, length us, event | category | flops | bytes accessed | tf_op | source)
XLA Modules:
  0.0 85.7 jit_solution(17406915633534855412)
XLA Ops:
  0.6 0.0 copy-start.1
  0.6 0.9 %copy-done.1 = f32[2,2,32,256]{3,2,1,0:T(8,128)S(1)} copy-done((f32[2,2,32,256]{3,2,1,0:T(8,128)S(1)}, f32[2,2,32,256]{3,2,1,0:T(8,128)}, u32[]{:S(2)}) %copy-start.1) | copy-done | bytes 131096
  1.6 11.7 %all_to_all.20 = f32[4,128,256]{2,1,0:T(8,128)S(1)} all-to-all(f32[4,128,256]{2,1,0:T(8,128)S(1)} %state_copies.1), channel_id=1, replica_groups={{0,1,2,3},{4,5,6,7},{8,9,10,11},{12,13,14,15},{16,20,24,28},{17,21,25,2..., dimensions={0} | all-to-all | bytes 1048576 | tf_op jit(solution)/shard_map/all_to_all | solution.py:339
  13.3 0.2 broadcast_in_dim.6
  13.5 0.0 copy-start
  13.5 0.0 copy-start.2
  13.5 0.0 copy-start.3
  13.6 0.0 copy-start.4
  13.6 0.0 copy-start.5
  13.6 0.0 copy-start.6
  13.6 0.0 copy-start.7
  13.6 19.5 %all_to_all.21 = f32[4,4,128,256]{3,2,1,0:T(8,128)S(1)} all-to-all(f32[4,4,128,256]{3,2,1,0:T(8,128)S(1)} %broadcast_in_dim.6), channel_id=1, replica_groups={{0,4,8,12},{1,5,9,13},{2,6,10,14},{3,7,11,15},{16,17,18,19},{20,21,22,2..., dimensions={0} | all-to-all | bytes 4194304 | tf_op jit(solution)/shard_map/all_to_all | solution.py:339
  33.1 0.0 copy-done
  33.1 0.0 copy-done.2
  33.1 0.0 copy-done.3
  33.1 0.0 copy-done.4
  33.1 0.0 copy-done.5
  33.1 0.0 copy-done.6
  33.2 0.0 copy-done.7
  33.2 1.3 %local_logits.1 = (f32[256,128]{1,0:T(8,128)S(1)}, f32[256,128]{1,0:T(8,128)S(1)}, f32[8,128]{1,0:T(8,128)S(1)}, f32[32,8,128]{2,1,0:T(8,128)S(1)}) custom-call(s32[2,2]{1,0:T(2,128)S(1)} %copy-done.4, f32[2,2]{1,0:T(2,128)S(1)} %copy-done.5, s32[1,2]{1,0:T(1,128)S(1)} %bitcast.16, f32[1,32]{1,0:T(1,128)S(1)} %bitcast.17, s32[2,2,32]{2,1,0:T(2,128)S(1)} %copy-done.2, ...), custom_call_target="tpu_custom_call" | custom-call | flops 805306368 | bytes 6291456 | tf_op jit(solution)/shard_map/local_logits/pallas_call | solution.py:186
  34.5 15.8 %all_to_all.22.stats_ref = f32[32,8,128]{2,1,0:T(8,128)S(1)} all-to-all(f32[32,8,128]{2,1,0:T(8,128)S(1)} %get-tuple-element.11), channel_id=1, replica_groups={{0,1,2,3,4,5,6,7,8,9,10,11,12,13,14,15,16,17,18,19,20,21,22,23,24,25,26..., dimensions={0} | all-to-all | bytes 262144 | tf_op jit(solution)/shard_map/all_to_all | solution.py:339
  50.3 2.4 %gradient_rows.1 = (f32[16,128,256]{2,1,0:T(8,128)}, f32[1,128]{1,0:T(1,128)S(1)}, f32[128,256]{1,0:T(8,128)S(1)}) custom-call(f32[32,8,128]{2,1,0:T(8,128)S(1)} %all_to_all.22.stats_ref, f32[8,128]{1,0:T(8,128)S(1)} %get-tuple-element.12.own_ref, f32[256,128]{1,0:T(8,128)S(1)} %get-tuple-element.13.scaled_ref, ...), custom_call_target="tpu_custom_call" | custom-call | flops 805306368 | bytes 6291456 | tf_op jit(solution)/shard_map/gradient_rows/pallas_call | solution.py:285
  52.7 3.7 %all-to-all-start.3 = ((f32[16,128,256]{2,1,0:T(8,128)}), f32[16,128,256]{2,1,0:T(8,128)S(1)}, u32[]{:S(2)}, u32[]{:S(2)}) async-start(f32[16,128,256]{2,1,0:T(8,128)} %get-tuple-element.15), calls=%async_computation.3 | async-start | bytes 4194304 | tf_op jit(solution)/shard_map/all_to_all | solution.py:339
  56.5 16.9 %all-gather.1 = f32[4,1,128]{2,1,0:T(1,128)S(1)} all-gather(f32[1,1,128]{2,1,0:T(1,128)S(1)} %bitcast.18), channel_id=1, replica_groups={{0,128,256,384},{1,129,257,385},{2,130,258,386},{3,131,259,387},{4,132,..., dimensions={0}, use_global_device_ids=true | all-gather | bytes 2560 | tf_op jit(solution)/shard_map/all_gather | solution.py:343
  73.4 8.0 %all-gather.2 = f32[4,1,128]{2,1,0:T(1,128)S(1)} all-gather(f32[1,1,128]{2,1,0:T(1,128)S(1)} %bitcast.19), channel_id=2, replica_groups={{0,32,64,96},{1,33,65,97},{2,34,66,98},{3,35,67,99},{4,36,68,100},{5,37..., dimensions={0}, use_global_device_ids=true | all-gather | bytes 2560 | tf_op jit(solution)/shard_map/all_gather | solution.py:343
  81.5 3.5 %all-to-all-done.3.parts_ref = f32[16,128,256]{2,1,0:T(8,128)S(1)} async-done(((f32[16,128,256]{2,1,0:T(8,128)}), f32[16,128,256]{2,1,0:T(8,128)S(1)}, u32[]{:S(2)}, u32[]{:S(2)}) %all-to-all-start.3) | async-done | bytes 2097184 | tf_op jit(solution)/shard_map/all_to_all | solution.py:339
  84.9 0.8 closing.1
  (2 shorter events, 0.1 us)
Async XLA Ops:
  0.6 0.9 %copy-start.1 = (f32[2,2,32,256]{3,2,1,0:T(8,128)S(1)}, f32[2,2,32,256]{3,2,1,0:T(8,128)}, u32[]{:S(2)}) copy-start(f32[2,2,32,256]{3,2,1,0:T(8,128)} %param.8) | copy-start | bytes 393220
  13.5 19.6 %copy-start = (f32[4096,256]{1,0:T(8,128)S(1)}, f32[4096,256]{1,0:T(8,128)}, u32[]{:S(2)}) copy-start(f32[4096,256]{1,0:T(8,128)} %param.9) | copy-start | bytes 12582916
  13.5 19.6 %copy-start.2 = (s32[2,2,32]{2,1,0:T(2,128)S(1)}, s32[2,2,32]{2,1,0:T(2,128)}, u32[]{:S(2)}) copy-start(s32[2,2,32]{2,1,0:T(2,128)} %targets_ref.1) | copy-start | bytes 1540
  13.5 19.6 %copy-start.3 = (f32[2,2,32]{2,1,0:T(2,128)S(1)}, f32[2,2,32]{2,1,0:T(2,128)}, u32[]{:S(2)}) copy-start(f32[2,2,32]{2,1,0:T(2,128)} %rest_lse_ref.1) | copy-start | bytes 1540
  13.6 19.6 %copy-start.4 = (s32[2,2]{1,0:T(2,128)S(1)}, s32[2,2]{1,0:T(2,128)}, u32[]{:S(2)}) copy-start(s32[2,2]{1,0:T(2,128)} %lengths_ref.1) | copy-start | bytes 52
  13.6 19.6 %copy-start.5 = (f32[2,2]{1,0:T(2,128)S(1)}, f32[2,2]{1,0:T(2,128)}, u32[]{:S(2)}) copy-start(f32[2,2]{1,0:T(2,128)} %ref_logp_ref.1) | copy-start | bytes 52
  13.6 19.6 %copy-start.6 = (s32[2]{0:T(128)S(1)}, s32[2]{0:T(128)}, u32[]{:S(2)}) copy-start(s32[2]{0:T(128)} %param.14) | copy-start | bytes 28
  13.6 19.6 %copy-start.7 = (f32[32]{0:T(128)S(1)}, f32[32]{0:T(128)}, u32[]{:S(2)}) copy-start(f32[32]{0:T(128)} %param.15) | copy-start | bytes 388
  52.7 32.2 %all-to-all-start.3 = ((f32[16,128,256]{2,1,0:T(8,128)}), f32[16,128,256]{2,1,0:T(8,128)S(1)}, u32[]{:S(2)}, u32[]{:S(2)}) async-start(f32[16,128,256]{2,1,0:T(8,128)} %get-tuple-element.15), calls=%async_computation.3 | async-start | bytes 4194304 | tf_op jit(solution)/shard_map/all_to_all | solution.py:339
